TPU v7x, 1024 devices: a whole 8x8x8 slice. The times are simulated.
1024 devices in a mesh: dp: 64 (over x, z), seq: 16 (over y, core).
Axes of the slice: x: 8, y: 8, z: 8, core: 2. Of those that a mesh axis runs over, the one named last changes fastest.
Arguments:
- spatial_qkv: bfloat16 [64, 3, 16, 128, 1152], P('dp', None, 'seq'), may hold values from -24 to 24
- temporal_qkv: bfloat16 [64, 3, 16, 128, 1152], P('dp', None, 'seq'), may hold values from -24 to 24
- cotangent: bfloat16 [64, 16, 128, 1152], P('dp', 'seq'), may hold values from -6 to 6
- spatial_gate: float32 [64, 1152], P('dp'), may hold values from -4 to 4
- temporal_gate: float32 [64, 1152], P('dp'), may hold values from -4 to 4
- temporal_proj: bfloat16 [1152, 1152], replicated, may hold values from -0.1875 to 0.1875
- live_counts: int32 [64, 2], P('dp'), may hold values from 2 to 128, as said below
Outputs:
- temporal_qkv_grad: bfloat16 [64, 3, 16, 128, 1152], P('dp', None, 'seq')
- spatial_proj_grad: float32 [1152, 1152], P('seq', 'dp')
- temporal_proj_grad: float32 [1152, 1152], P('seq', 'dp')
Inputs may be any that keep to these rules, and one draw needn't show every extreme that they name: live_counts[g, 0] counts a clip's live frames, at most 16; live_counts[g, 1] counts the live positions of each of its frames, at most 128; in every draw some clip has all 16 frames and all 128 positions live.
All inputs are finite; a program needn't handle non-finite values.
Results may differ from a plain program's by a relative error of at most 0.015.
Values may be sent and summed in bfloat16 or wider, within the bound.
No kernel may reach another device: no remote copies, remote signals or barrier semaphores. Data moves between devices by JAX's collectives and lax.ppermute only.
A program may use at most 64 MiB of HBM per device.

v0:
```python
import jax
import jax.numpy as jnp
from jax import lax
from jax.experimental import pallas as pl
from jax.experimental.pallas import tpu as pltpu
from jax.sharding import PartitionSpec as P


HEADS = 16
HD = 72
LANES = 128
HALF = 640
SCALE = HD ** (-0.5)
NN = (((1,), (0,)), ((), ()))
NT = (((1,), (1,)), ((), ()))
TN = (((0,), (0,)), ((), ()))


def dot(left, right, dims):
    return lax.dot_general(left, right, dims, preferred_element_type=jnp.float32)


def head_tiles(head):
    return head * HD // LANES, ((head + 1) * HD + LANES - 1) // LANES


def head_lanes(head, first, last):
    lane = lax.broadcasted_iota(jnp.int32, (1, (last - first) * LANES), 1) + first * LANES
    return (lane >= head * HD) & (lane < (head + 1) * HD)


class Rows:
    def __init__(self, store):
        self.store = store
        self.open = {}

    def add(self, head, first, last, value, keep):
        for tile in range(first, last):
            at = slice((tile - first) * LANES, (tile - first + 1) * LANES)
            piece = value[:, at]
            if tile in self.open:
                piece = jnp.where(keep[:, at], piece, self.open[tile])
            self.open[tile] = piece
        done = (head + 1) * HD // LANES
        for tile in [t for t in self.open if t < done]:
            self.store(tile, self.open.pop(tile))


def softmax(scores):
    expo = jnp.exp(scores - jnp.max(scores, axis=-1, keepdims=True))
    return expo / jnp.sum(expo, axis=-1, keepdims=True)


def hand_over(core, out, error, mine, send):
    width = out.shape[-1]
    low, high = slice(0, HALF), slice(width - HALF, width)

    @pl.when(core == 0)
    def _():
        mine[...] = out[:, low]
        send[:, :HALF] = out[:, high]

    @pl.when(core == 1)
    def _():
        mine[...] = out[:, high]
        send[:, :HALF] = out[:, low]

    send[:, HALF:] = error


def spatial_kernel(counts, qkv, incoming, gate, mine, send, out):
    tokens, _ = incoming.shape
    member = lax.axis_index("seq")
    live_positions = counts[0, 1]
    keys_live = lax.broadcasted_iota(jnp.int32, (1, tokens), 1) < live_positions

    def store(tile, value):
        out[:, tile * LANES : (tile + 1) * LANES] = value.astype(jnp.bfloat16)

    rows = Rows(store)
    for head in range(HEADS):
        first, last = head_tiles(head)
        keep = head_lanes(head, first, last)
        at = slice(first * LANES, last * LANES)
        queries = jnp.where(keep, qkv[0, :, at], 0)
        scores = dot(queries, qkv[1, :, at], NT) * SCALE
        weights = softmax(jnp.where(keys_live, scores, -1e30)).astype(jnp.bfloat16)
        rows.add(head, first, last, dot(weights, qkv[2, :, at], NN), keep)
    token = lax.broadcasted_iota(jnp.int32, (tokens, 1), 0)
    live = ((token < live_positions) & (member < counts[0, 0])).astype(jnp.float32)
    error = (live * incoming[...].astype(jnp.float32) * gate[...]).astype(jnp.bfloat16)
    hand_over(member % 2, out, error, mine, send)


class Block:
    def __init__(self, counts, arrived):
        self.arrived = arrived
        self.frames, rows, self.width = arrived.shape
        self.positions = rows // 4
        self.tokens = self.frames * self.positions
        query = lax.broadcasted_iota(jnp.int32, (self.tokens, self.tokens), 0)
        key = lax.broadcasted_iota(jnp.int32, (self.tokens, self.tokens), 1)
        same = query % self.positions == key % self.positions
        self.pairs = same & (key // self.positions < counts[0, 0])

    def load(self, which, at=slice(None)):
        block = self.arrived[:, which * self.positions : (which + 1) * self.positions, at]
        return block.reshape(self.tokens, block.shape[-1])

    def weights(self, at, keep):
        scores = dot(jnp.where(keep, self.load(0, at), 0), self.load(1, at), NT) * SCALE
        return softmax(jnp.where(self.pairs, scores, -1e30))


def forward_kernel(counts, arrived, gate, mine, send, out):
    block = Block(counts, arrived)
    member = lax.axis_index("seq")

    def store(tile, value):
        out[:, tile * LANES : (tile + 1) * LANES] = value.astype(jnp.bfloat16)

    rows = Rows(store)
    for head in range(HEADS):
        first, last = head_tiles(head)
        keep = head_lanes(head, first, last)
        at = slice(first * LANES, last * LANES)
        weights = block.weights(at, keep).astype(jnp.bfloat16)
        rows.add(head, first, last, dot(weights, block.load(2, at), NN), keep)
    token = lax.broadcasted_iota(jnp.int32, (block.tokens, 1), 0)
    place = token % block.positions + member * block.positions
    live = (token // block.positions < counts[0, 0]) & (place < counts[0, 1])
    flowing = live.astype(jnp.float32) * block.load(3).astype(jnp.float32)
    hand_over(member % 2, out, (flowing * gate[...]).astype(jnp.bfloat16), mine, send)


def backward_kernel(counts, arrived, send, proj, grads, back):
    block = Block(counts, arrived)
    back[...] = dot(send[:, HALF:], proj[...], NT).astype(jnp.bfloat16)

    def into(which):
        rows = slice(which * block.positions, (which + 1) * block.positions)

        def store(tile, value):
            value = value.reshape(block.frames, block.positions, LANES).astype(jnp.bfloat16)
            grads[:, rows, tile * LANES : (tile + 1) * LANES] = value

        return Rows(store)

    to_q, to_k, to_v = into(0), into(1), into(2)
    for head in range(HEADS):
        first, last = head_tiles(head)
        keep = head_lanes(head, first, last)
        at = slice(first * LANES, last * LANES)
        weights = block.weights(at, keep)
        b = back[:, at]
        to_v.add(head, first, last, dot(weights.astype(jnp.bfloat16), b, TN), keep)
        reaching = dot(jnp.where(keep, b, 0), block.load(2, at), NT)
        reaching = reaching.astype(jnp.bfloat16).astype(jnp.float32)
        drop = jnp.sum(reaching * weights, axis=-1, keepdims=True)
        slope = (weights * (reaching - drop) * SCALE).astype(jnp.bfloat16)
        to_q.add(head, first, last, dot(slope, block.load(1, at), NN), keep)
        to_k.add(head, first, last, dot(slope, block.load(0, at), TN), keep)


def part_kernel(mine, send, came, part):
    total = dot(send[:, HALF:], mine[...], TN) + dot(came[:, HALF:], came[:, :HALF], TN)
    part[...] = total.astype(jnp.bfloat16).reshape(part.shape)


SM = pl.BlockSpec(memory_space=pltpu.SMEM)
VM = pl.BlockSpec(memory_space=pltpu.VMEM)


def shape(*dims):
    return jax.ShapeDtypeStruct(dims, jnp.bfloat16)


def cost(flops):
    return pl.CostEstimate(flops=flops, transcendentals=0, bytes_accessed=4_000_000)


def lines(major):
    side = round(lax.axis_size("dp") ** 0.5)
    if major:
        return [[x * side + z for x in range(side)] for z in range(side)]
    return [[x * side + z for z in range(side)] for x in range(side)]


def exchange(blocks, axis, groups=None):
    return lax.all_to_all(blocks, axis, split_axis=0, concat_axis=0, tiled=True, axis_index_groups=groups)


def shifts(blocks, axis, here, peers, to):
    came = [lax.dynamic_index_in_dim(blocks, here, 0, keepdims=False)]
    count = lax.axis_size(axis)
    for step in range(1, peers):
        block = lax.dynamic_index_in_dim(blocks, (here + step) % peers, 0, keepdims=False)
        came.append(lax.ppermute(block, axis, [(i, to(i, step)) for i in range(count)]))
    return came


def summed(blocks):
    total = blocks[0].astype(jnp.float32)
    for block in blocks[1:]:
        total = total + block.astype(jnp.float32)
    return total


def part_of(mine, send):
    width = send.shape[1] - HALF
    side = len(lines(True))
    came = lax.ppermute(send, "seq", [(i, i ^ 1) for i in range(lax.axis_size("seq"))])
    return pl.pallas_call(
        part_kernel,
        in_specs=[VM] * 3,
        out_specs=VM,
        out_shape=shape(side, width // side, HALF),
        cost_estimate=cost(2_000_000_000),
        name="part",
    )(mine, send, came)


def body(spatial_qkv, temporal_qkv, cotangent, spatial_gate, temporal_gate, temporal_proj, live_counts):
    peers = lax.axis_size("seq")
    member = lax.axis_index("seq")
    core = member % 2
    incoming = cotangent[0, 0]
    tokens, width = incoming.shape
    positions = tokens // peers
    side = len(lines(True))
    x, z = lax.axis_index("dp") // side, lax.axis_index("dp") % side
    along_x = lambda i, n: (i // side + n) % side * side + i % side
    along_z = lambda i, n: i // side * side + (i % side + n) % side
    blocks = jnp.concatenate([temporal_qkv[0, :, 0], cotangent[0]]).reshape(4, peers, positions, width)
    blocks = jnp.moveaxis(blocks, 1, 0).reshape(peers, 4 * positions, width)
    arrived = exchange(blocks, "seq")
    handed = [shape(tokens, HALF), shape(tokens, HALF + width)]
    kept_out = [pltpu.VMEM((tokens, width), jnp.bfloat16)]
    mine_s, send_s = pl.pallas_call(
        spatial_kernel,
        in_specs=[SM, VM, VM, VM],
        out_specs=[VM] * 2,
        out_shape=handed,
        scratch_shapes=kept_out,
        cost_estimate=cost(4_000_000_000),
        name="spatial",
    )(live_counts, spatial_qkv[0, :, 0], incoming, spatial_gate)
    part_s = part_of(mine_s, send_s)
    came_s = shifts(part_s, "dp", x, side, along_x)
    mine_t, send_t = pl.pallas_call(
        forward_kernel,
        in_specs=[SM, VM, VM],
        out_specs=[VM] * 2,
        out_shape=handed,
        scratch_shapes=kept_out,
        cost_estimate=cost(4_000_000_000),
        name="forward",
    )(live_counts, arrived, temporal_gate)
    part_t = part_of(mine_t, send_t)
    came_t = shifts(part_t, "dp", x, side, along_x)
    grads = pl.pallas_call(
        backward_kernel,
        in_specs=[SM, VM, VM, VM],
        out_specs=VM,
        out_shape=shape(peers, 3 * positions, width),
        scratch_shapes=kept_out,
        cost_estimate=cost(8_000_000_000),
        name="backward",
    )(live_counts, arrived, send_t, temporal_proj)
    home = exchange(grads, "seq")
    sums = jnp.concatenate([summed(came_s), summed(came_t)], axis=1).astype(jnp.bfloat16)
    came = shifts(sums.reshape(side, -1, 2 * HALF), "dp", z, side, along_z)
    both = summed(came).reshape(-1, 2, HALF)
    kept = HEADS * HD // 2
    heads = jnp.where(core == 0, both[:, :, :kept], both[:, :, HALF - kept :])
    heads = heads.reshape(-1, 2, HEADS // 2, HD).transpose(2, 1, 0, 3)
    heads = jnp.concatenate([jnp.where(core == 0, heads, 0), jnp.where(core == 1, heads, 0)])
    home, heads = lax.optimization_barrier((home, heads))
    home = jnp.moveaxis(home.reshape(peers, 3, positions, width), 1, 0).reshape(3, 1, tokens, width)
    rows = exchange(heads.reshape(HEADS, -1, HD), "seq").sum(axis=0).reshape(2, -1, HD)
    return (home[None], rows[0].T, rows[1].T)


def solution(mesh):
    return jax.shard_map(
        body,
        mesh=mesh,
        in_specs=(
            P("dp", None, "seq", None, None),
            P("dp", None, "seq", None, None),
            P("dp", "seq", None, None),
            P("dp", None),
            P("dp", None),
            P(),
            P("dp", None),
        ),
        out_specs=(P("dp", None, "seq", None, None), P("seq", "dp"), P("seq", "dp")),
        check_vma=False,
    )
```

profile of v0, /device:TPU:1, one launch (start us, length us, event | category | flops | bytes accessed | tf_op | source)
XLA Modules:
  0.0 228.2 jit_solution(9723688710754690659)
XLA Ops:
  3.9 17.6 %all-to-all-start = ((bf16[16,32,1152]{2,1,0:T(8,128)(2,1)}), bf16[16,32,1152]{2,1,0:T(8,128)(2,1)S(1)}, u32[]{:S(2)}, u32[]{:S(2)}) async-start(bf16[16,32,1152]{2,1,0:T(8,128)(2,1)} %maximum_bitcast_fusion), calls=%async_computation | async-start | bytes 2359296 | tf_op jit(solution)/shard_map/all_to_all | solution.py:190
  21.5 5.6 %spatial.1 = (bf16[128,640]{1,0:T(8,128)(2,1)}, bf16[128,1792]{1,0:T(8,128)(2,1)}) custom-call(s32[1,2]{1,0:T(1,128)} %counts.5, bf16[3,128,1152]{2,1,0:T(8,128)(2,1)} %bitcast.83, bf16[128,1152]{1,0:T(8,128)(2,1)} %bitcast.82, f32[1,1152]{1,0:T(1,128)} %gate.3), custom_call_target="tpu_custom_call" | custom-call | flops 4000000000 | bytes 4000000 | tf_op jit(solution)/shard_map/spatial/pallas_call | solution.py:239
  29.2 23.0 %all-to-all-done.arrived = bf16[16,32,1152]{2,1,0:T(8,128)(2,1)S(1)} async-done(((bf16[16,32,1152]{2,1,0:T(8,128)(2,1)}), bf16[16,32,1152]{2,1,0:T(8,128)(2,1)S(1)}, u32[]{:S(2)}, u32[]{:S(2)}) %all-to-all-start) | async-done | bytes 1179680 | tf_op jit(solution)/shard_map/all_to_all | solution.py:190
  53.2 5.6 %forward.1 = (bf16[128,640]{1,0:T(8,128)(2,1)}, bf16[128,1792]{1,0:T(8,128)(2,1)}) custom-call(s32[1,2]{1,0:T(1,128)} %counts.5, bf16[16,32,1152]{2,1,0:T(8,128)(2,1)} %copy-done.1, f32[1,1152]{1,0:T(1,128)} %gate.2), custom_call_target="tpu_custom_call" | custom-call | flops 4000000000 | bytes 4000000 | tf_op jit(solution)/shard_map/forward/pallas_call | solution.py:250
  61.8 3.3 %part.2 = bf16[8,144,640]{2,1,0:T(8,128)(2,1)} custom-call(bf16[128,640]{1,0:T(8,128)(2,1)} %get-tuple-element.10.mine, bf16[128,1792]{1,0:T(8,128)(2,1)} %get-tuple-element.11.send, bf16[128,1792]{1,0:T(8,128)(2,1)} %copy-done.4), custom_call_target="tpu_custom_call" | custom-call | flops 2000000000 | bytes 4000000 | tf_op jit(solution)/shard_map/part/pallas_call | solution.py:213
  73.1 7.5 %collective-permute-start.4 = (bf16[144,640]{1,0:T(8,128)(2,1)S(1)}, bf16[144,640]{1,0:T(8,128)(2,1)S(1)}, u32[]{:S(2)}, u32[]{:S(2)}) collective-permute-start(bf16[144,640]{1,0:T(8,128)(2,1)S(1)} %get-tuple-element.26), channel_id=1, source_target_pairs={{0,512},{16,528},{32,544},{48,560},{64,576},{80,592},{96,608},{112... | collective-permute-start | bytes 552968 | tf_op jit(solution)/shard_map/ppermute | solution.py:198
  82.6 3.4 %part.3 = bf16[8,144,640]{2,1,0:T(8,128)(2,1)} custom-call(bf16[128,640]{1,0:T(8,128)(2,1)} %get-tuple-element.12.mine, bf16[128,1792]{1,0:T(8,128)(2,1)} %get-tuple-element.9.send, bf16[128,1792]{1,0:T(8,128)(2,1)} %copy-done.3), custom_call_target="tpu_custom_call" | custom-call | flops 2000000000 | bytes 4000000 | tf_op jit(solution)/shard_map/part/pallas_call | solution.py:213
  88.4 4.2 %collective-permute-start.2 = (bf16[144,640]{1,0:T(8,128)(2,1)}, bf16[144,640]{1,0:T(8,128)(2,1)S(1)}, u32[]{:S(2)}, u32[]{:S(2)}) collective-permute-start(bf16[144,640]{1,0:T(8,128)(2,1)} %get-tuple-element.28), channel_id=1, source_target_pairs={{0,256},{16,272},{32,288},{48,304},{64,320},{80,336},{96,352},{112... | collective-permute-start | bytes 552968 | tf_op jit(solution)/shard_map/ppermute | solution.py:198
  94.9 4.3 %collective-permute-start.15 = (bf16[144,640]{1,0:T(8,128)(2,1)}, bf16[144,640]{1,0:T(8,128)(2,1)S(1)}, u32[]{:S(2)}, u32[]{:S(2)}) collective-permute-start(bf16[144,640]{1,0:T(8,128)(2,1)} %get-tuple-element.16), channel_id=1, source_target_pairs={{0,896},{16,912},{32,928},{48,944},{64,960},{80,976},{96,992},{112... | collective-permute-start | bytes 552968 | tf_op jit(solution)/shard_map/ppermute | solution.py:198
  99.2 4.3 %collective-permute-start.14 = (bf16[144,640]{1,0:T(8,128)(2,1)}, bf16[144,640]{1,0:T(8,128)(2,1)S(1)}, u32[]{:S(2)}, u32[]{:S(2)}) collective-permute-start(bf16[144,640]{1,0:T(8,128)(2,1)} %get-tuple-element.17), channel_id=1, source_target_pairs={{0,768},{16,784},{32,800},{48,816},{64,832},{80,848},{96,864},{112... | collective-permute-start | bytes 552968 | tf_op jit(solution)/shard_map/ppermute | solution.py:198
  103.5 11.8 %backward.1 = bf16[16,24,1152]{2,1,0:T(8,128)(2,1)} custom-call(s32[1,2]{1,0:T(1,128)} %counts.5, bf16[16,32,1152]{2,1,0:T(8,128)(2,1)} %copy-done.1, bf16[128,1792]{1,0:T(8,128)(2,1)} %get-tuple-element.9.send, bf16[1152,1152]{1,0:T(8,128)(2,1)} %proj.1), custom_call_target="tpu_custom_call" | custom-call | flops 8000000000 | bytes 4000000 | tf_op jit(solution)/shard_map/backward/pallas_call | solution.py:261
  115.3 10.2 %all-to-all-start.1 = ((bf16[16,24,1152]{2,1,0:T(8,128)(2,1)}), bf16[16,24,1152]{2,1,0:T(8,128)(2,1)S(1)}, u32[]{:S(2)}, u32[]{:S(2)}) async-start(bf16[16,24,1152]{2,1,0:T(8,128)(2,1)} %backward.1), calls=%async_computation.1 | async-start | bytes 1769472 | tf_op jit(solution)/shard_map/all_to_all | solution.py:190
  128.3 6.4 %collective-permute-start.12 = (bf16[144,640]{1,0:T(8,128)(2,1)}, bf16[144,640]{1,0:T(8,128)(2,1)}, u32[]{:S(2)}, u32[]{:S(2)}) collective-permute-start(bf16[144,640]{1,0:T(8,128)(2,1)} %get-tuple-element.19), channel_id=1, source_target_pairs={{0,512},{16,528},{32,544},{48,560},{64,576},{80,592},{96,608},{112... | collective-permute-start | bytes 552968 | tf_op jit(solution)/shard_map/ppermute | solution.py:198
  136.7 3.6 %collective-permute-start.10 = (bf16[144,640]{1,0:T(8,128)(2,1)}, bf16[144,640]{1,0:T(8,128)(2,1)}, u32[]{:S(2)}, u32[]{:S(2)}) collective-permute-start(bf16[144,640]{1,0:T(8,128)(2,1)} %get-tuple-element.21), channel_id=1, source_target_pairs={{0,256},{16,272},{32,288},{48,304},{64,320},{80,336},{96,352},{112... | collective-permute-start | bytes 552968 | tf_op jit(solution)/shard_map/ppermute | solution.py:198
  140.3 3.9 %collective-permute-start.9 = (bf16[144,640]{1,0:T(8,128)(2,1)}, bf16[144,640]{1,0:T(8,128)(2,1)}, u32[]{:S(2)}, u32[]{:S(2)}) collective-permute-start(bf16[144,640]{1,0:T(8,128)(2,1)} %get-tuple-element.15), channel_id=1, source_target_pairs={{0,128},{16,144},{32,160},{48,176},{64,192},{80,208},{96,224},{112... | collective-permute-start | bytes 552968 | tf_op jit(solution)/shard_map/ppermute | solution.py:198
  148.3 15.8 %collective-permute-done.10 = bf16[144,640]{1,0:T(8,128)(2,1)} collective-permute-done((bf16[144,640]{1,0:T(8,128)(2,1)}, bf16[144,640]{1,0:T(8,128)(2,1)}, u32[]{:S(2)}, u32[]{:S(2)}) %collective-permute-start.10) | collective-permute-done | bytes 184352 | tf_op jit(solution)/shard_map/ppermute | solution.py:198
  164.1 4.8 %collective-permute-done.9 = bf16[144,640]{1,0:T(8,128)(2,1)} collective-permute-done((bf16[144,640]{1,0:T(8,128)(2,1)}, bf16[144,640]{1,0:T(8,128)(2,1)}, u32[]{:S(2)}, u32[]{:S(2)}) %collective-permute-start.9) | collective-permute-done | bytes 184352 | tf_op jit(solution)/shard_map/ppermute | solution.py:198
  170.5 9.6 %collective-permute-start.22 = (bf16[18,1280]{1,0:T(8,128)(2,1)S(1)}, bf16[18,1280]{1,0:T(8,128)(2,1)S(1)}, u32[]{:S(2)}, u32[]{:S(2)}) collective-permute-start(bf16[18,1280]{1,0:T(8,128)(2,1)S(1)} %get-tuple-element.30), channel_id=1, source_target_pairs={{0,112},{16,0},{32,16},{48,32},{64,48},{80,64},{96,80},{112,96},{1... | collective-permute-start | bytes 138248 | tf_op jit(solution)/shard_map/ppermute | solution.py:198
  184.0 7.3 %collective-permute-start.19 = (bf16[18,1280]{1,0:T(8,128)(2,1)S(1)}, bf16[18,1280]{1,0:T(8,128)(2,1)S(1)}, u32[]{:S(2)}, u32[]{:S(2)}) collective-permute-start(bf16[18,1280]{1,0:T(8,128)(2,1)S(1)} %get-tuple-element.33), channel_id=1, source_target_pairs={{0,64},{16,80},{32,96},{48,112},{64,0},{80,16},{96,32},{112,48},{1... | collective-permute-start | bytes 138248 | tf_op jit(solution)/shard_map/ppermute | solution.py:198
  193.2 3.4 %collective-permute-start.17 = (bf16[18,1280]{1,0:T(8,128)(2,1)S(1)}, bf16[18,1280]{1,0:T(8,128)(2,1)S(1)}, u32[]{:S(2)}, u32[]{:S(2)}) collective-permute-start(bf16[18,1280]{1,0:T(8,128)(2,1)S(1)} %get-tuple-element.35), channel_id=1, source_target_pairs={{0,32},{16,48},{32,64},{48,80},{64,96},{80,112},{96,0},{112,16},{1... | collective-permute-start | bytes 138248 | tf_op jit(solution)/shard_map/ppermute | solution.py:198
  196.6 3.1 %collective-permute-start.16 = (bf16[18,1280]{1,0:T(8,128)(2,1)S(1)}, bf16[18,1280]{1,0:T(8,128)(2,1)S(1)}, u32[]{:S(2)}, u32[]{:S(2)}) collective-permute-start(bf16[18,1280]{1,0:T(8,128)(2,1)S(1)} %get-tuple-element.29), channel_id=1, source_target_pairs={{0,16},{16,32},{32,48},{48,64},{64,80},{80,96},{96,112},{112,0},{1... | collective-permute-start | bytes 138248 | tf_op jit(solution)/shard_map/ppermute | solution.py:198
  199.9 3.7 %collective-permute-done.17 = bf16[18,1280]{1,0:T(8,128)(2,1)S(1)} collective-permute-done((bf16[18,1280]{1,0:T(8,128)(2,1)S(1)}, bf16[18,1280]{1,0:T(8,128)(2,1)S(1)}, u32[]{:S(2)}, u32[]{:S(2)}) %collective-permute-start.17) | collective-permute-done | bytes 46112 | tf_op jit(solution)/shard_map/ppermute | solution.py:198
  206.6 8.1 %all-to-all-start.2 = ((f32[16,36,72]{2,1,0:T(8,128)}), f32[16,36,72]{2,1,0:T(8,128)S(1)}, u32[]{:S(2)}, u32[]{:S(2)}) async-start(f32[16,36,72]{2,1,0:T(8,128)} %copy.26), calls=%async_computation.2 | async-start | bytes 655360 | tf_op jit(solution)/shard_map/all_to_all | solution.py:190
  215.6 12.0 %all-to-all-done.2 = f32[16,36,72]{2,1,0:T(8,128)S(1)} async-done(((f32[16,36,72]{2,1,0:T(8,128)}), f32[16,36,72]{2,1,0:T(8,128)S(1)}, u32[]{:S(2)}, u32[]{:S(2)}) %all-to-all-start.2) | async-done | bytes 165920 | tf_op jit(solution)/shard_map/all_to_all | solution.py:190
  (64 shorter events, 44.5 us)
Async XLA Ops:
  3.9 48.3 %all-to-all-start = ((bf16[16,32,1152]{2,1,0:T(8,128)(2,1)}), bf16[16,32,1152]{2,1,0:T(8,128)(2,1)S(1)}, u32[]{:S(2)}, u32[]{:S(2)}) async-start(bf16[16,32,1152]{2,1,0:T(8,128)(2,1)} %maximum_bitcast_fusion), calls=%async_computation | async-start | bytes 2359296 | tf_op jit(solution)/shard_map/all_to_all | solution.py:190
  27.1 33.9 %collective-permute-start = (bf16[128,1792]{1,0:T(8,128)(2,1)}, bf16[128,1792]{1,0:T(8,128)(2,1)S(1)}, u32[]{:S(2)}, u32[]{:S(2)}) collective-permute-start(bf16[128,1792]{1,0:T(8,128)(2,1)} %get-tuple-element.11.send), channel_id=1, source_target_pairs={{0,1},{1,0},{2,3},{3,2},{4,5},{5,4},{6,7},{7,6},{8,9},{9,8},{10,11... | collective-permute-start | bytes 1376264 | tf_op jit(solution)/shard_map/ppermute | solution.py:212
  58.8 21.9 %collective-permute-start.8 = (bf16[128,1792]{1,0:T(8,128)(2,1)}, bf16[128,1792]{1,0:T(8,128)(2,1)S(1)}, u32[]{:S(2)}, u32[]{:S(2)}) collective-permute-start(bf16[128,1792]{1,0:T(8,128)(2,1)} %get-tuple-element.9.send), channel_id=1, source_target_pairs={{0,1},{1,0},{2,3},{3,2},{4,5},{5,4},{6,7},{7,6},{8,9},{9,8},{10,11... | collective-permute-start | bytes 1376264 | tf_op jit(solution)/shard_map/ppermute | solution.py:212
  67.3 21.1 %collective-permute-start.7 = (bf16[144,640]{1,0:T(8,128)(2,1)S(1)}, bf16[144,640]{1,0:T(8,128)(2,1)S(1)}, u32[]{:S(2)}, u32[]{:S(2)}) collective-permute-start(bf16[144,640]{1,0:T(8,128)(2,1)S(1)} %get-tuple-element.23), channel_id=1, source_target_pairs={{0,896},{16,912},{32,928},{48,944},{64,960},{80,976},{96,992},{112... | collective-permute-start | bytes 552968 | tf_op jit(solution)/shard_map/ppermute | solution.py:198
  69.3 23.4 %collective-permute-start.6 = (bf16[144,640]{1,0:T(8,128)(2,1)S(1)}, bf16[144,640]{1,0:T(8,128)(2,1)S(1)}, u32[]{:S(2)}, u32[]{:S(2)}) collective-permute-start(bf16[144,640]{1,0:T(8,128)(2,1)S(1)} %get-tuple-element.24), channel_id=1, source_target_pairs={{0,768},{16,784},{32,800},{48,816},{64,832},{80,848},{96,864},{112... | collective-permute-start | bytes 552968 | tf_op jit(solution)/shard_map/ppermute | solution.py:198
  71.2 23.7 %collective-permute-start.5 = (bf16[144,640]{1,0:T(8,128)(2,1)S(1)}, bf16[144,640]{1,0:T(8,128)(2,1)S(1)}, u32[]{:S(2)}, u32[]{:S(2)}) collective-permute-start(bf16[144,640]{1,0:T(8,128)(2,1)S(1)} %get-tuple-element.25), channel_id=1, source_target_pairs={{0,640},{16,656},{32,672},{48,688},{64,704},{80,720},{96,736},{112... | collective-permute-start | bytes 552968 | tf_op jit(solution)/shard_map/ppermute | solution.py:198
  73.1 26.1 %collective-permute-start.4 = (bf16[144,640]{1,0:T(8,128)(2,1)S(1)}, bf16[144,640]{1,0:T(8,128)(2,1)S(1)}, u32[]{:S(2)}, u32[]{:S(2)}) collective-permute-start(bf16[144,640]{1,0:T(8,128)(2,1)S(1)} %get-tuple-element.26), channel_id=1, source_target_pairs={{0,512},{16,528},{32,544},{48,560},{64,576},{80,592},{96,608},{112... | collective-permute-start | bytes 552968 | tf_op jit(solution)/shard_map/ppermute | solution.py:198
  80.7 44.8 %collective-permute-start.3 = (bf16[144,640]{1,0:T(8,128)(2,1)}, bf16[144,640]{1,0:T(8,128)(2,1)S(1)}, u32[]{:S(2)}, u32[]{:S(2)}) collective-permute-start(bf16[144,640]{1,0:T(8,128)(2,1)} %get-tuple-element.27), channel_id=1, source_target_pairs={{0,384},{16,400},{32,416},{48,432},{64,448},{80,464},{96,480},{112... | collective-permute-start | bytes 552968 | tf_op jit(solution)/shard_map/ppermute | solution.py:198
  88.4 39.8 %collective-permute-start.2 = (bf16[144,640]{1,0:T(8,128)(2,1)}, bf16[144,640]{1,0:T(8,128)(2,1)S(1)}, u32[]{:S(2)}, u32[]{:S(2)}) collective-permute-start(bf16[144,640]{1,0:T(8,128)(2,1)} %get-tuple-element.28), channel_id=1, source_target_pairs={{0,256},{16,272},{32,288},{48,304},{64,320},{80,336},{96,352},{112... | collective-permute-start | bytes 552968 | tf_op jit(solution)/shard_map/ppermute | solution.py:198
  92.7 42.0 %collective-permute-start.1 = (bf16[144,640]{1,0:T(8,128)(2,1)}, bf16[144,640]{1,0:T(8,128)(2,1)S(1)}, u32[]{:S(2)}, u32[]{:S(2)}) collective-permute-start(bf16[144,640]{1,0:T(8,128)(2,1)} %get-tuple-element.22), channel_id=1, source_target_pairs={{0,128},{16,144},{32,160},{48,176},{64,192},{80,208},{96,224},{112... | collective-permute-start | bytes 552968 | tf_op jit(solution)/shard_map/ppermute | solution.py:198
  94.9 41.7 %collective-permute-start.15 = (bf16[144,640]{1,0:T(8,128)(2,1)}, bf16[144,640]{1,0:T(8,128)(2,1)S(1)}, u32[]{:S(2)}, u32[]{:S(2)}) collective-permute-start(bf16[144,640]{1,0:T(8,128)(2,1)} %get-tuple-element.16), channel_id=1, source_target_pairs={{0,896},{16,912},{32,928},{48,944},{64,960},{80,976},{96,992},{112... | collective-permute-start | bytes 552968 | tf_op jit(solution)/shard_map/ppermute | solution.py:198
  99.2 41.1 %collective-permute-start.14 = (bf16[144,640]{1,0:T(8,128)(2,1)}, bf16[144,640]{1,0:T(8,128)(2,1)S(1)}, u32[]{:S(2)}, u32[]{:S(2)}) collective-permute-start(bf16[144,640]{1,0:T(8,128)(2,1)} %get-tuple-element.17), channel_id=1, source_target_pairs={{0,768},{16,784},{32,800},{48,816},{64,832},{80,848},{96,864},{112... | collective-permute-start | bytes 552968 | tf_op jit(solution)/shard_map/ppermute | solution.py:198
  115.3 90.4 %all-to-all-start.1 = ((bf16[16,24,1152]{2,1,0:T(8,128)(2,1)}), bf16[16,24,1152]{2,1,0:T(8,128)(2,1)S(1)}, u32[]{:S(2)}, u32[]{:S(2)}) async-start(bf16[16,24,1152]{2,1,0:T(8,128)(2,1)} %backward.1), calls=%async_computation.1 | async-start | bytes 1769472 | tf_op jit(solution)/shard_map/all_to_all | solution.py:190
  125.5 20.1 %collective-permute-start.13 = (bf16[144,640]{1,0:T(8,128)(2,1)}, bf16[144,640]{1,0:T(8,128)(2,1)}, u32[]{:S(2)}, u32[]{:S(2)}) collective-permute-start(bf16[144,640]{1,0:T(8,128)(2,1)} %get-tuple-element.18), channel_id=1, source_target_pairs={{0,640},{16,656},{32,672},{48,688},{64,704},{80,720},{96,736},{112... | collective-permute-start | bytes 552968 | tf_op jit(solution)/shard_map/ppermute | solution.py:198
  128.3 20.0 %collective-permute-start.12 = (bf16[144,640]{1,0:T(8,128)(2,1)}, bf16[144,640]{1,0:T(8,128)(2,1)}, u32[]{:S(2)}, u32[]{:S(2)}) collective-permute-start(bf16[144,640]{1,0:T(8,128)(2,1)} %get-tuple-element.19), channel_id=1, source_target_pairs={{0,512},{16,528},{32,544},{48,560},{64,576},{80,592},{96,608},{112... | collective-permute-start | bytes 552968 | tf_op jit(solution)/shard_map/ppermute | solution.py:198
  134.7 13.6 %collective-permute-start.11 = (bf16[144,640]{1,0:T(8,128)(2,1)}, bf16[144,640]{1,0:T(8,128)(2,1)}, u32[]{:S(2)}, u32[]{:S(2)}) collective-permute-start(bf16[144,640]{1,0:T(8,128)(2,1)} %get-tuple-element.20), channel_id=1, source_target_pairs={{0,384},{16,400},{32,416},{48,432},{64,448},{80,464},{96,480},{112... | collective-permute-start | bytes 552968 | tf_op jit(solution)/shard_map/ppermute | solution.py:198
  136.7 27.4 %collective-permute-start.10 = (bf16[144,640]{1,0:T(8,128)(2,1)}, bf16[144,640]{1,0:T(8,128)(2,1)}, u32[]{:S(2)}, u32[]{:S(2)}) collective-permute-start(bf16[144,640]{1,0:T(8,128)(2,1)} %get-tuple-element.21), channel_id=1, source_target_pairs={{0,256},{16,272},{32,288},{48,304},{64,320},{80,336},{96,352},{112... | collective-permute-start | bytes 552968 | tf_op jit(solution)/shard_map/ppermute | solution.py:198
  140.3 28.5 %collective-permute-start.9 = (bf16[144,640]{1,0:T(8,128)(2,1)}, bf16[144,640]{1,0:T(8,128)(2,1)}, u32[]{:S(2)}, u32[]{:S(2)}) collective-permute-start(bf16[144,640]{1,0:T(8,128)(2,1)} %get-tuple-element.15), channel_id=1, source_target_pairs={{0,128},{16,144},{32,160},{48,176},{64,192},{80,208},{96,224},{112... | collective-permute-start | bytes 552968 | tf_op jit(solution)/shard_map/ppermute | solution.py:198
  170.5 22.6 %collective-permute-start.22 = (bf16[18,1280]{1,0:T(8,128)(2,1)S(1)}, bf16[18,1280]{1,0:T(8,128)(2,1)S(1)}, u32[]{:S(2)}, u32[]{:S(2)}) collective-permute-start(bf16[18,1280]{1,0:T(8,128)(2,1)S(1)} %get-tuple-element.30), channel_id=1, source_target_pairs={{0,112},{16,0},{32,16},{48,32},{64,48},{80,64},{96,80},{112,96},{1... | collective-permute-start | bytes 138248 | tf_op jit(solution)/shard_map/ppermute | solution.py:198
  180.1 16.4 %collective-permute-start.21 = (bf16[18,1280]{1,0:T(8,128)(2,1)S(1)}, bf16[18,1280]{1,0:T(8,128)(2,1)S(1)}, u32[]{:S(2)}, u32[]{:S(2)}) collective-permute-start(bf16[18,1280]{1,0:T(8,128)(2,1)S(1)} %get-tuple-element.31), channel_id=1, source_target_pairs={{0,96},{16,112},{32,0},{48,16},{64,32},{80,48},{96,64},{112,80},{1... | collective-permute-start | bytes 138248 | tf_op jit(solution)/shard_map/ppermute | solution.py:198
  182.0 17.6 %collective-permute-start.20 = (bf16[18,1280]{1,0:T(8,128)(2,1)S(1)}, bf16[18,1280]{1,0:T(8,128)(2,1)S(1)}, u32[]{:S(2)}, u32[]{:S(2)}) collective-permute-start(bf16[18,1280]{1,0:T(8,128)(2,1)S(1)} %get-tuple-element.32), channel_id=1, source_target_pairs={{0,80},{16,96},{32,112},{48,0},{64,16},{80,32},{96,48},{112,64},{1... | collective-permute-start | bytes 138248 | tf_op jit(solution)/shard_map/ppermute | solution.py:198
  184.0 15.7 %collective-permute-start.19 = (bf16[18,1280]{1,0:T(8,128)(2,1)S(1)}, bf16[18,1280]{1,0:T(8,128)(2,1)S(1)}, u32[]{:S(2)}, u32[]{:S(2)}) collective-permute-start(bf16[18,1280]{1,0:T(8,128)(2,1)S(1)} %get-tuple-element.33), channel_id=1, source_target_pairs={{0,64},{16,80},{32,96},{48,112},{64,0},{80,16},{96,32},{112,48},{1... | collective-permute-start | bytes 138248 | tf_op jit(solution)/shard_map/ppermute | solution.py:198
  193.2 10.4 %collective-permute-start.17 = (bf16[18,1280]{1,0:T(8,128)(2,1)S(1)}, bf16[18,1280]{1,0:T(8,128)(2,1)S(1)}, u32[]{:S(2)}, u32[]{:S(2)}) collective-permute-start(bf16[18,1280]{1,0:T(8,128)(2,1)S(1)} %get-tuple-element.35), channel_id=1, source_target_pairs={{0,32},{16,48},{32,64},{48,80},{64,96},{80,112},{96,0},{112,16},{1... | collective-permute-start | bytes 138248 | tf_op jit(solution)/shard_map/ppermute | solution.py:198
  206.6 21.0 %all-to-all-start.2 = ((f32[16,36,72]{2,1,0:T(8,128)}), f32[16,36,72]{2,1,0:T(8,128)S(1)}, u32[]{:S(2)}, u32[]{:S(2)}) async-start(f32[16,36,72]{2,1,0:T(8,128)} %copy.26), calls=%async_computation.2 | async-start | bytes 655360 | tf_op jit(solution)/shard_map/all_to_all | solution.py:190
  (7 other events, 27.7 us)
where the time goes:
time: 230 us; the launch traced here: 228 us
  starting transfers between devices  118 us (51%)
  waiting for transfers between devices  63.6 us (28%)
  Pallas kernels  29.6 us (13%)
  local copies, waits for them, and re-layouts  10.7 us (5%)
  other arithmetic  5.13 us (2%)
    ppermute x21, starting transfers between devices, shifts(): lax.ppermute(block, axis, [(i, to(i, step)) for i in range(count)])  78 us
    all_to_all x3, starting transfers between devices, exchange(): lax.all_to_all(blocks, axis, split_axis=0, concat_axis=0, tiled=True, axi...  35.9 us
    all_to_all x3, waiting for transfers between devices, exchange(): lax.all_to_all(blocks, axis, split_axis=0, concat_axis=0, tiled=True, axi...  35 us
    ppermute x21, waiting for transfers between devices, shifts(): lax.ppermute(block, axis, [(i, to(i, step)) for i in range(count)])  28.7 us
    pallas_call x1, Pallas kernels, body(): pl.pallas_call(backward_kernel, in_specs=[SM, VM, VM, VM], out_specs=VM,...  11.8 us
    pallas_call x2, Pallas kernels, part_of(): pl.pallas_call(part_kernel, in_specs=[VM] * 3, out_specs=VM, out_shape=sh...  6.67 us
    pallas_call x1, Pallas kernels, body(): pl.pallas_call(spatial_kernel, in_specs=[SM, VM, VM, VM], out_specs=[VM]...  5.58 us
    pallas_call x1, Pallas kernels, body(): pl.pallas_call(forward_kernel, in_specs=[SM, VM, VM], out_specs=[VM] * 2,...  5.56 us
  transfers between devices with their start and end apart: 26, of which 8 were waited for; matrix products, arithmetic and copies ran while one was open for 4% of the time, Pallas kernels for 13%

commit v1 on v0

--- a/solution.py
+++ b/solution.py
@@ -46,25 +46,39 @@
             self.store(tile, self.open.pop(tile))
 
 
+class Shares:
+    def __init__(self, shares):
+        self.shares = shares
+        self.open = {}
+
+    def add(self, head, first, last, value, keep):
+        value = jnp.where(keep, value, 0)
+        if last - first == 1:
+            value = jnp.concatenate([value, jnp.zeros_like(value)], axis=1)
+        core, slot = head % 2, head // 2
+        goal = slot * HD // LANES
+        shift = (slot * HD - goal * LANES) - (head * HD - first * LANES)
+        if shift:
+            value = pltpu.roll(value, shift % (2 * LANES), 1)
+        for tile in range(goal, ((slot + 1) * HD + LANES - 1) // LANES):
+            piece = value[:, (tile - goal) * LANES : (tile - goal + 1) * LANES]
+            if (core, tile) in self.open:
+                piece = piece + self.open[core, tile]
+            self.open[core, tile] = piece
+        done = (slot + 1) * HD // LANES if slot + 1 < HEADS // 2 else HALF // LANES
+        for key in [k for k in self.open if k[0] == core and k[1] < done]:
+            lanes = slice(key[1] * LANES, (key[1] + 1) * LANES)
+            self.shares[core, :, lanes] = self.open.pop(key).astype(jnp.bfloat16)
+
+
 def softmax(scores):
     expo = jnp.exp(scores - jnp.max(scores, axis=-1, keepdims=True))
     return expo / jnp.sum(expo, axis=-1, keepdims=True)
 
 
-def hand_over(core, out, error, mine, send):
-    width = out.shape[-1]
-    low, high = slice(0, HALF), slice(width - HALF, width)
-
-    @pl.when(core == 0)
-    def _():
-        mine[...] = out[:, low]
-        send[:, :HALF] = out[:, high]
-
-    @pl.when(core == 1)
-    def _():
-        mine[...] = out[:, high]
-        send[:, :HALF] = out[:, low]
-
+def hand_over(core, shares, error, mine, send):
+    mine[...] = shares[core]
+    send[:, :HALF] = shares[1 - core]
     send[:, HALF:] = error
 
 
@@ -74,10 +88,7 @@
     live_positions = counts[0, 1]
     keys_live = lax.broadcasted_iota(jnp.int32, (1, tokens), 1) < live_positions
 
-    def store(tile, value):
-        out[:, tile * LANES : (tile + 1) * LANES] = value.astype(jnp.bfloat16)
-
-    rows = Rows(store)
+    rows = Shares(out)
     for head in range(HEADS):
         first, last = head_tiles(head)
         keep = head_lanes(head, first, last)
@@ -116,10 +127,7 @@
     block = Block(counts, arrived)
     member = lax.axis_index("seq")
 
-    def store(tile, value):
-        out[:, tile * LANES : (tile + 1) * LANES] = value.astype(jnp.bfloat16)
-
-    rows = Rows(store)
+    rows = Shares(out)
     for head in range(HEADS):
         first, last = head_tiles(head)
         keep = head_lanes(head, first, last)
@@ -186,6 +194,10 @@
     return [[x * side + z for z in range(side)] for x in range(side)]
 
 
+def near(array):
+    return pltpu.with_memory_space_constraint(array, pltpu.VMEM)
+
+
 def exchange(blocks, axis, groups=None):
     return lax.all_to_all(blocks, axis, split_axis=0, concat_axis=0, tiled=True, axis_index_groups=groups)
 
@@ -222,8 +234,6 @@
 
 def body(spatial_qkv, temporal_qkv, cotangent, spatial_gate, temporal_gate, temporal_proj, live_counts):
     peers = lax.axis_size("seq")
-    member = lax.axis_index("seq")
-    core = member % 2
     incoming = cotangent[0, 0]
     tokens, width = incoming.shape
     positions = tokens // peers
@@ -233,18 +243,18 @@
     along_z = lambda i, n: i // side * side + (i % side + n) % side
     blocks = jnp.concatenate([temporal_qkv[0, :, 0], cotangent[0]]).reshape(4, peers, positions, width)
     blocks = jnp.moveaxis(blocks, 1, 0).reshape(peers, 4 * positions, width)
-    arrived = exchange(blocks, "seq")
+    arrived = near(exchange(blocks, "seq"))
     handed = [shape(tokens, HALF), shape(tokens, HALF + width)]
-    kept_out = [pltpu.VMEM((tokens, width), jnp.bfloat16)]
+    shares = [pltpu.VMEM((2, tokens, HALF), jnp.bfloat16)]
     mine_s, send_s = pl.pallas_call(
         spatial_kernel,
         in_specs=[SM, VM, VM, VM],
         out_specs=[VM] * 2,
         out_shape=handed,
-        scratch_shapes=kept_out,
+        scratch_shapes=shares,
         cost_estimate=cost(4_000_000_000),
         name="spatial",
-    )(live_counts, spatial_qkv[0, :, 0], incoming, spatial_gate)
+    )(live_counts, near(spatial_qkv[0, :, 0]), near(incoming), spatial_gate)
     part_s = part_of(mine_s, send_s)
     came_s = shifts(part_s, "dp", x, side, along_x)
     mine_t, send_t = pl.pallas_call(
@@ -252,32 +262,33 @@
         in_specs=[SM, VM, VM],
         out_specs=[VM] * 2,
         out_shape=handed,
-        scratch_shapes=kept_out,
+        scratch_shapes=shares,
         cost_estimate=cost(4_000_000_000),
         name="forward",
     )(live_counts, arrived, temporal_gate)
     part_t = part_of(mine_t, send_t)
-    came_t = shifts(part_t, "dp", x, side, along_x)
+    came_t = exchange(part_t, "dp", lines(True))
     grads = pl.pallas_call(
         backward_kernel,
         in_specs=[SM, VM, VM, VM],
         out_specs=VM,
         out_shape=shape(peers, 3 * positions, width),
-        scratch_shapes=kept_out,
+        scratch_shapes=[pltpu.VMEM((tokens, width), jnp.bfloat16)],
         cost_estimate=cost(8_000_000_000),
         name="backward",
     )(live_counts, arrived, send_t, temporal_proj)
+    came_t, grads = lax.optimization_barrier((came_t, grads))
     home = exchange(grads, "seq")
-    sums = jnp.concatenate([summed(came_s), summed(came_t)], axis=1).astype(jnp.bfloat16)
+    sum_t = summed([came_t[i] for i in range(side)])
+    sums = jnp.concatenate([summed(came_s), sum_t], axis=1).astype(jnp.bfloat16)
     came = shifts(sums.reshape(side, -1, 2 * HALF), "dp", z, side, along_z)
     both = summed(came).reshape(-1, 2, HALF)
-    kept = HEADS * HD // 2
-    heads = jnp.where(core == 0, both[:, :, :kept], both[:, :, HALF - kept :])
-    heads = heads.reshape(-1, 2, HEADS // 2, HD).transpose(2, 1, 0, 3)
-    heads = jnp.concatenate([jnp.where(core == 0, heads, 0), jnp.where(core == 1, heads, 0)])
+    heads = both[:, :, : HEADS // 2 * HD].reshape(-1, 2, HEADS // 2, HD).transpose(2, 1, 0, 3)
+    heads = heads.reshape(HEADS // 2, -1, HD)
     home, heads = lax.optimization_barrier((home, heads))
     home = jnp.moveaxis(home.reshape(peers, 3, positions, width), 1, 0).reshape(3, 1, tokens, width)
-    rows = exchange(heads.reshape(HEADS, -1, HD), "seq").sum(axis=0).reshape(2, -1, HD)
+    chips = [[i for i in range(peers) if i % 2 == c] for c in range(2)]
+    rows = exchange(heads, "seq", chips).sum(axis=0).reshape(2, -1, HD)
     return (home[None], rows[0].T, rows[1].T)
 
 

time: 230 us -> 194 us (0.84)
  the two profiles are of different devices: /device:TPU:1 before, /device:TPU:14 now
where the time goes in v1:
time: 194 us; the launch traced here: 193 us
  starting transfers between devices  88.7 us (46%)
  blocking collectives  38.6 us (20%)
  Pallas kernels  28.4 us (15%)
  waiting for transfers between devices  24.6 us (13%)
  local copies, waits for them, and re-layouts  7.73 us (4%)
  other arithmetic  3.89 us (2%)
    ppermute x14, starting transfers between devices, shifts(): lax.ppermute(block, axis, [(i, to(i, step)) for i in range(count)])  61 us
    all_to_all x1, blocking collectives, exchange(): lax.all_to_all(blocks, axis, split_axis=0, concat_axis=0, tiled=True, axi...  38.6 us
    all_to_all x3, starting transfers between devices, exchange(): lax.all_to_all(blocks, axis, split_axis=0, concat_axis=0, tiled=True, axi...  23.1 us
    ppermute x14, waiting for transfers between devices, shifts(): lax.ppermute(block, axis, [(i, to(i, step)) for i in range(count)])  12.8 us
    pallas_call x1, Pallas kernels, body(): pl.pallas_call(backward_kernel, in_specs=[SM, VM, VM, VM], out_specs=VM,...  11.4 us
    all_to_all x3, waiting for transfers between devices, exchange(): lax.all_to_all(blocks, axis, split_axis=0, concat_axis=0, tiled=True, axi...  8.45 us
    pallas_call x2, Pallas kernels, part_of(): pl.pallas_call(part_kernel, in_specs=[VM] * 3, out_specs=VM, out_shape=sh...  6.63 us
    pallas_call x1, Pallas kernels, body(): pl.pallas_call(spatial_kernel, in_specs=[SM, VM, VM, VM], out_specs=[VM]...  5.2 us
  transfers between devices with their start and end apart: 19, of which 7 were waited for; matrix products, arithmetic and copies ran while one was open for 3% of the time, Pallas kernels for 10%

profile of v1, /device:TPU:14, one launch (start us, length us, event | category | flops | bytes accessed | tf_op | source)
XLA Modules:
  0.0 193.2 jit_solution(16500378968488640549)
XLA Ops:
  2.9 38.6 %all_to_all.20.arrived = bf16[16,32,1152]{2,1,0:T(8,128)(2,1)S(1)} all-to-all(bf16[16,32,1152]{2,1,0:T(8,128)(2,1)S(1)} %maximum_bitcast_fusion), channel_id=1, replica_groups=mesh['dp'=64,'seq'=16] {'seq'}, dimensions={0} | all-to-all | bytes 2359296 | tf_op jit(solution)/shard_map/all_to_all | solution.py:202
  41.5 5.1 %forward.1 = (bf16[128,640]{1,0:T(8,128)(2,1)}, bf16[128,1792]{1,0:T(8,128)(2,1)}) custom-call(s32[1,2]{1,0:T(1,128)} %counts.5, bf16[16,32,1152]{2,1,0:T(8,128)(2,1)S(1)} %all_to_all.20.arrived, f32[1,1152]{1,0:T(1,128)} %gate.2), custom_call_target="tpu_custom_call" | custom-call | flops 4000000000 | bytes 4000000 | tf_op jit(solution)/shard_map/forward/pallas_call | solution.py:260
  51.6 3.3 %part.2 = bf16[8,144,640]{2,1,0:T(8,128)(2,1)} custom-call(bf16[128,640]{1,0:T(8,128)(2,1)} %get-tuple-element.11.mine, bf16[128,1792]{1,0:T(8,128)(2,1)} %get-tuple-element.12.send, bf16[128,1792]{1,0:T(8,128)(2,1)} %copy-done.4), custom_call_target="tpu_custom_call" | custom-call | flops 2000000000 | bytes 4000000 | tf_op jit(solution)/shard_map/part/pallas_call | solution.py:225
  54.9 12.6 %all-to-all-start.1 = ((bf16[8,144,640]{2,1,0:T(8,128)(2,1)}), bf16[8,144,640]{2,1,0:T(8,128)(2,1)}, u32[]{:S(2)}, u32[]{:S(2)}) async-start(bf16[8,144,640]{2,1,0:T(8,128)(2,1)} %part.2), calls=%async_computation.1 | async-start | bytes 2949120 | tf_op jit(solution)/shard_map/all_to_all | solution.py:202
  67.5 5.2 %spatial.1 = (bf16[128,640]{1,0:T(8,128)(2,1)}, bf16[128,1792]{1,0:T(8,128)(2,1)}) custom-call(s32[1,2]{1,0:T(1,128)} %counts.5, bf16[3,128,1152]{2,1,0:T(8,128)(2,1)S(1)} %bitcast.63, bf16[128,1152]{1,0:T(8,128)(2,1)S(1)} %bitcast.62, f32[1,1152]{1,0:T(1,128)} %gate.3), custom_call_target="tpu_custom_call" | custom-call | flops 4000000000 | bytes 4000000 | tf_op jit(solution)/shard_map/spatial/pallas_call | solution.py:249
  77.4 3.3 %part.3 = bf16[8,144,640]{2,1,0:T(8,128)(2,1)} custom-call(bf16[128,640]{1,0:T(8,128)(2,1)} %get-tuple-element.14.mine, bf16[128,1792]{1,0:T(8,128)(2,1)} %get-tuple-element.15.send, bf16[128,1792]{1,0:T(8,128)(2,1)} %copy-done.3), custom_call_target="tpu_custom_call" | custom-call | flops 2000000000 | bytes 4000000 | tf_op jit(solution)/shard_map/part/pallas_call | solution.py:225
  85.0 4.7 %collective-permute-start.3 = (bf16[144,640]{1,0:T(8,128)(2,1)S(1)}, bf16[144,640]{1,0:T(8,128)(2,1)S(1)}, u32[]{:S(2)}, u32[]{:S(2)}) collective-permute-start(bf16[144,640]{1,0:T(8,128)(2,1)S(1)} %get-tuple-element.25), channel_id=1, source_target_pairs={{0,256},{16,272},{32,288},{48,304},{64,320},{80,336},{96,352},{112... | collective-permute-start | bytes 552968 | tf_op jit(solution)/shard_map/ppermute | solution.py:210
  89.7 5.5 %collective-permute-start.4 = (bf16[144,640]{1,0:T(8,128)(2,1)}, bf16[144,640]{1,0:T(8,128)(2,1)S(1)}, u32[]{:S(2)}, u32[]{:S(2)}) collective-permute-start(bf16[144,640]{1,0:T(8,128)(2,1)} %get-tuple-element.24), channel_id=1, source_target_pairs={{0,384},{16,400},{32,416},{48,432},{64,448},{80,464},{96,480},{112... | collective-permute-start | bytes 552968 | tf_op jit(solution)/shard_map/ppermute | solution.py:210
  95.3 3.3 %collective-permute-start.5 = (bf16[144,640]{1,0:T(8,128)(2,1)}, bf16[144,640]{1,0:T(8,128)(2,1)S(1)}, u32[]{:S(2)}, u32[]{:S(2)}) collective-permute-start(bf16[144,640]{1,0:T(8,128)(2,1)} %get-tuple-element.23), channel_id=1, source_target_pairs={{0,512},{16,528},{32,544},{48,560},{64,576},{80,592},{96,608},{112... | collective-permute-start | bytes 552968 | tf_op jit(solution)/shard_map/ppermute | solution.py:210
  98.6 4.3 %collective-permute-start.6 = (bf16[144,640]{1,0:T(8,128)(2,1)}, bf16[144,640]{1,0:T(8,128)(2,1)S(1)}, u32[]{:S(2)}, u32[]{:S(2)}) collective-permute-start(bf16[144,640]{1,0:T(8,128)(2,1)} %get-tuple-element.22), channel_id=1, source_target_pairs={{0,640},{16,656},{32,672},{48,688},{64,704},{80,720},{96,736},{112... | collective-permute-start | bytes 552968 | tf_op jit(solution)/shard_map/ppermute | solution.py:210
  102.9 3.9 %collective-permute-done.2 = bf16[144,640]{1,0:T(8,128)(2,1)S(1)} collective-permute-done((bf16[144,640]{1,0:T(8,128)(2,1)S(1)}, bf16[144,640]{1,0:T(8,128)(2,1)S(1)}, u32[]{:S(2)}, u32[]{:S(2)}) %collective-permute-start.2) | collective-permute-done | bytes 184352 | tf_op jit(solution)/shard_map/ppermute | solution.py:210
  106.8 3.4 %collective-permute-start.7 = (bf16[144,640]{1,0:T(8,128)(2,1)}, bf16[144,640]{1,0:T(8,128)(2,1)S(1)}, u32[]{:S(2)}, u32[]{:S(2)}) collective-permute-start(bf16[144,640]{1,0:T(8,128)(2,1)} %get-tuple-element.21), channel_id=1, source_target_pairs={{0,768},{16,784},{32,800},{48,816},{64,832},{80,848},{96,864},{112... | collective-permute-start | bytes 552968 | tf_op jit(solution)/shard_map/ppermute | solution.py:210
  110.2 5.0 %collective-permute-done.3 = bf16[144,640]{1,0:T(8,128)(2,1)S(1)} collective-permute-done((bf16[144,640]{1,0:T(8,128)(2,1)S(1)}, bf16[144,640]{1,0:T(8,128)(2,1)S(1)}, u32[]{:S(2)}, u32[]{:S(2)}) %collective-permute-start.3) | collective-permute-done | bytes 184352 | tf_op jit(solution)/shard_map/ppermute | solution.py:210
  115.2 5.2 %collective-permute-start.8 = (bf16[144,640]{1,0:T(8,128)(2,1)S(1)}, bf16[144,640]{1,0:T(8,128)(2,1)S(1)}, u32[]{:S(2)}, u32[]{:S(2)}) collective-permute-start(bf16[144,640]{1,0:T(8,128)(2,1)S(1)} %get-tuple-element.20), channel_id=1, source_target_pairs={{0,896},{16,912},{32,928},{48,944},{64,960},{80,976},{96,992},{112... | collective-permute-start | bytes 552968 | tf_op jit(solution)/shard_map/ppermute | solution.py:210
  120.4 11.4 %backward.1 = bf16[16,24,1152]{2,1,0:T(8,128)(2,1)} custom-call(s32[1,2]{1,0:T(1,128)} %counts.5, bf16[16,32,1152]{2,1,0:T(8,128)(2,1)S(1)} %all_to_all.20.arrived, bf16[128,1792]{1,0:T(8,128)(2,1)} %get-tuple-element.12.send, bf16[1152,1152]{1,0:T(8,128)(2,1)} %proj.1), custom_call_target="tpu_custom_call" | custom-call | flops 8000000000 | bytes 4000000 | tf_op jit(solution)/shard_map/backward/pallas_call | solution.py:271
  131.8 3.6 %all-to-all-start.2 = ((bf16[16,24,1152]{2,1,0:T(8,128)(2,1)}), bf16[16,24,1152]{2,1,0:T(8,128)(2,1)S(1)}, u32[]{:S(2)}, u32[]{:S(2)}) async-start(bf16[16,24,1152]{2,1,0:T(8,128)(2,1)} %backward.1), calls=%async_computation.2 | async-start | bytes 1769472 | tf_op jit(solution)/shard_map/all_to_all | solution.py:202
  140.9 10.9 %collective-permute-start.11 = (bf16[18,1280]{1,0:T(8,128)(2,1)S(1)}, bf16[18,1280]{1,0:T(8,128)(2,1)S(1)}, u32[]{:S(2)}, u32[]{:S(2)}) collective-permute-start(bf16[18,1280]{1,0:T(8,128)(2,1)S(1)} %get-tuple-element.31), channel_id=1, source_target_pairs={{0,48},{16,64},{32,80},{48,96},{64,112},{80,0},{96,16},{112,32},{1... | collective-permute-start | bytes 138248 | tf_op jit(solution)/shard_map/ppermute | solution.py:210
  151.8 5.6 %collective-permute-start.12 = (bf16[18,1280]{1,0:T(8,128)(2,1)S(1)}, bf16[18,1280]{1,0:T(8,128)(2,1)S(1)}, u32[]{:S(2)}, u32[]{:S(2)}) collective-permute-start(bf16[18,1280]{1,0:T(8,128)(2,1)S(1)} %get-tuple-element.30), channel_id=1, source_target_pairs={{0,64},{16,80},{32,96},{48,112},{64,0},{80,16},{96,32},{112,48},{1... | collective-permute-start | bytes 138248 | tf_op jit(solution)/shard_map/ppermute | solution.py:210
  157.4 5.1 %collective-permute-start.13 = (bf16[18,1280]{1,0:T(8,128)(2,1)S(1)}, bf16[18,1280]{1,0:T(8,128)(2,1)S(1)}, u32[]{:S(2)}, u32[]{:S(2)}) collective-permute-start(bf16[18,1280]{1,0:T(8,128)(2,1)S(1)} %get-tuple-element.29), channel_id=1, source_target_pairs={{0,80},{16,96},{32,112},{48,0},{64,16},{80,32},{96,48},{112,64},{1... | collective-permute-start | bytes 138248 | tf_op jit(solution)/shard_map/ppermute | solution.py:210
  162.5 2.8 %collective-permute-start.14 = (bf16[18,1280]{1,0:T(8,128)(2,1)S(1)}, bf16[18,1280]{1,0:T(8,128)(2,1)S(1)}, u32[]{:S(2)}, u32[]{:S(2)}) collective-permute-start(bf16[18,1280]{1,0:T(8,128)(2,1)S(1)} %get-tuple-element.28), channel_id=1, source_target_pairs={{0,96},{16,112},{32,0},{48,16},{64,32},{80,48},{96,64},{112,80},{1... | collective-permute-start | bytes 138248 | tf_op jit(solution)/shard_map/ppermute | solution.py:210
  167.9 3.4 %collective-permute-start.9 = (bf16[18,1280]{1,0:T(8,128)(2,1)S(1)}, bf16[18,1280]{1,0:T(8,128)(2,1)S(1)}, u32[]{:S(2)}, u32[]{:S(2)}) collective-permute-start(bf16[18,1280]{1,0:T(8,128)(2,1)S(1)} %get-tuple-element.26), channel_id=1, source_target_pairs={{0,16},{16,32},{32,48},{48,64},{64,80},{80,96},{96,112},{112,0},{1... | collective-permute-start | bytes 138248 | tf_op jit(solution)/shard_map/ppermute | solution.py:210
  171.6 3.6 %collective-permute-done.9 = bf16[18,1280]{1,0:T(8,128)(2,1)S(1)} collective-permute-done((bf16[18,1280]{1,0:T(8,128)(2,1)S(1)}, bf16[18,1280]{1,0:T(8,128)(2,1)S(1)}, u32[]{:S(2)}, u32[]{:S(2)}) %collective-permute-start.9) | collective-permute-done | bytes 46112 | tf_op jit(solution)/shard_map/ppermute | solution.py:210
  176.2 6.9 %all-to-all-start.3 = ((f32[8,36,72]{2,1,0:T(8,128)}), f32[8,36,72]{2,1,0:T(8,128)S(1)}, u32[]{:S(2)}, u32[]{:S(2)}) async-start(f32[8,36,72]{2,1,0:T(8,128)} %copy.25), calls=%async_computation.3 | async-start | bytes 327680 | tf_op jit(solution)/shard_map/all_to_all | solution.py:202
  184.1 8.4 %all-to-all-done.3 = f32[8,36,72]{2,1,0:T(8,128)S(1)} async-done(((f32[8,36,72]{2,1,0:T(8,128)}), f32[8,36,72]{2,1,0:T(8,128)S(1)}, u32[]{:S(2)}, u32[]{:S(2)}) %all-to-all-start.3) | async-done | bytes 82976 | tf_op jit(solution)/shard_map/all_to_all | solution.py:202
  (47 shorter events, 26.6 us)
Async XLA Ops:
  0.6 1.2 copy-start
  46.6 4.2 %collective-permute-start = (bf16[128,1792]{1,0:T(8,128)(2,1)}, bf16[128,1792]{1,0:T(8,128)(2,1)S(1)}, u32[]{:S(2)}, u32[]{:S(2)}) collective-permute-start(bf16[128,1792]{1,0:T(8,128)(2,1)} %get-tuple-element.12.send), channel_id=1, source_target_pairs={{0,1},{1,0},{2,3},{3,2},{4,5},{5,4},{6,7},{7,6},{8,9},{9,8},{10,11... | collective-permute-start | bytes 1376264 | tf_op jit(solution)/shard_map/ppermute | solution.py:224
  50.8 0.8 copy-start.4
  54.9 12.6 %copy-start.1 = (bf16[1,1,128,1152]{3,2,1,0:T(8,128)(2,1)S(1)}, bf16[1,1,128,1152]{3,2,1,0:T(8,128)(2,1)}, u32[]{:S(2)}) copy-start(bf16[1,1,128,1152]{3,2,1,0:T(8,128)(2,1)} %param.9) | copy-start | bytes 884740
  54.9 12.6 %copy-start.2 = (bf16[1,3,1,128,1152]{4,3,2,1,0:T(8,128)(2,1)S(1)}, bf16[1,3,1,128,1152]{4,3,2,1,0:T(8,128)(2,1)}, u32[]{:S(2)}) copy-start(bf16[1,3,1,128,1152]{4,3,2,1,0:T(8,128)(2,1)} %param.7) | copy-start | bytes 2654212
  54.9 76.8 %all-to-all-start.1 = ((bf16[8,144,640]{2,1,0:T(8,128)(2,1)}), bf16[8,144,640]{2,1,0:T(8,128)(2,1)}, u32[]{:S(2)}, u32[]{:S(2)}) async-start(bf16[8,144,640]{2,1,0:T(8,128)(2,1)} %part.2), calls=%async_computation.1 | async-start | bytes 2949120 | tf_op jit(solution)/shard_map/all_to_all | solution.py:202
  72.7 3.9 %collective-permute-start.1 = (bf16[128,1792]{1,0:T(8,128)(2,1)}, bf16[128,1792]{1,0:T(8,128)(2,1)S(1)}, u32[]{:S(2)}, u32[]{:S(2)}) collective-permute-start(bf16[128,1792]{1,0:T(8,128)(2,1)} %get-tuple-element.15.send), channel_id=1, source_target_pairs={{0,1},{1,0},{2,3},{3,2},{4,5},{5,4},{6,7},{7,6},{8,9},{9,8},{10,11... | collective-permute-start | bytes 1376264 | tf_op jit(solution)/shard_map/ppermute | solution.py:224
  76.6 0.8 copy-start.3
  83.0 23.8 %collective-permute-start.2 = (bf16[144,640]{1,0:T(8,128)(2,1)S(1)}, bf16[144,640]{1,0:T(8,128)(2,1)S(1)}, u32[]{:S(2)}, u32[]{:S(2)}) collective-permute-start(bf16[144,640]{1,0:T(8,128)(2,1)S(1)} %get-tuple-element.19), channel_id=1, source_target_pairs={{0,128},{16,144},{32,160},{48,176},{64,192},{80,208},{96,224},{112... | collective-permute-start | bytes 552968 | tf_op jit(solution)/shard_map/ppermute | solution.py:210
  85.0 30.1 %collective-permute-start.3 = (bf16[144,640]{1,0:T(8,128)(2,1)S(1)}, bf16[144,640]{1,0:T(8,128)(2,1)S(1)}, u32[]{:S(2)}, u32[]{:S(2)}) collective-permute-start(bf16[144,640]{1,0:T(8,128)(2,1)S(1)} %get-tuple-element.25), channel_id=1, source_target_pairs={{0,256},{16,272},{32,288},{48,304},{64,320},{80,336},{96,352},{112... | collective-permute-start | bytes 552968 | tf_op jit(solution)/shard_map/ppermute | solution.py:210
  89.7 45.8 %collective-permute-start.4 = (bf16[144,640]{1,0:T(8,128)(2,1)}, bf16[144,640]{1,0:T(8,128)(2,1)S(1)}, u32[]{:S(2)}, u32[]{:S(2)}) collective-permute-start(bf16[144,640]{1,0:T(8,128)(2,1)} %get-tuple-element.24), channel_id=1, source_target_pairs={{0,384},{16,400},{32,416},{48,432},{64,448},{80,464},{96,480},{112... | collective-permute-start | bytes 552968 | tf_op jit(solution)/shard_map/ppermute | solution.py:210
  95.3 40.3 %collective-permute-start.5 = (bf16[144,640]{1,0:T(8,128)(2,1)}, bf16[144,640]{1,0:T(8,128)(2,1)S(1)}, u32[]{:S(2)}, u32[]{:S(2)}) collective-permute-start(bf16[144,640]{1,0:T(8,128)(2,1)} %get-tuple-element.23), channel_id=1, source_target_pairs={{0,512},{16,528},{32,544},{48,560},{64,576},{80,592},{96,608},{112... | collective-permute-start | bytes 552968 | tf_op jit(solution)/shard_map/ppermute | solution.py:210
  98.6 37.0 %collective-permute-start.6 = (bf16[144,640]{1,0:T(8,128)(2,1)}, bf16[144,640]{1,0:T(8,128)(2,1)S(1)}, u32[]{:S(2)}, u32[]{:S(2)}) collective-permute-start(bf16[144,640]{1,0:T(8,128)(2,1)} %get-tuple-element.22), channel_id=1, source_target_pairs={{0,640},{16,656},{32,672},{48,688},{64,704},{80,720},{96,736},{112... | collective-permute-start | bytes 552968 | tf_op jit(solution)/shard_map/ppermute | solution.py:210
  106.8 28.8 %collective-permute-start.7 = (bf16[144,640]{1,0:T(8,128)(2,1)}, bf16[144,640]{1,0:T(8,128)(2,1)S(1)}, u32[]{:S(2)}, u32[]{:S(2)}) collective-permute-start(bf16[144,640]{1,0:T(8,128)(2,1)} %get-tuple-element.21), channel_id=1, source_target_pairs={{0,768},{16,784},{32,800},{48,816},{64,832},{80,848},{96,864},{112... | collective-permute-start | bytes 552968 | tf_op jit(solution)/shard_map/ppermute | solution.py:210
  115.2 20.4 %collective-permute-start.8 = (bf16[144,640]{1,0:T(8,128)(2,1)S(1)}, bf16[144,640]{1,0:T(8,128)(2,1)S(1)}, u32[]{:S(2)}, u32[]{:S(2)}) collective-permute-start(bf16[144,640]{1,0:T(8,128)(2,1)S(1)} %get-tuple-element.20), channel_id=1, source_target_pairs={{0,896},{16,912},{32,928},{48,944},{64,960},{80,976},{96,992},{112... | collective-permute-start | bytes 552968 | tf_op jit(solution)/shard_map/ppermute | solution.py:210
  131.8 43.7 %all-to-all-start.2 = ((bf16[16,24,1152]{2,1,0:T(8,128)(2,1)}), bf16[16,24,1152]{2,1,0:T(8,128)(2,1)S(1)}, u32[]{:S(2)}, u32[]{:S(2)}) async-start(bf16[16,24,1152]{2,1,0:T(8,128)(2,1)} %backward.1), calls=%async_computation.2 | async-start | bytes 1769472 | tf_op jit(solution)/shard_map/all_to_all | solution.py:202
  138.6 26.8 %collective-permute-start.10 = (bf16[18,1280]{1,0:T(8,128)(2,1)S(1)}, bf16[18,1280]{1,0:T(8,128)(2,1)S(1)}, u32[]{:S(2)}, u32[]{:S(2)}) collective-permute-start(bf16[18,1280]{1,0:T(8,128)(2,1)S(1)} %get-tuple-element.32), channel_id=1, source_target_pairs={{0,32},{16,48},{32,64},{48,80},{64,96},{80,112},{96,0},{112,16},{1... | collective-permute-start | bytes 138248 | tf_op jit(solution)/shard_map/ppermute | solution.py:210
  140.9 27.0 %collective-permute-start.11 = (bf16[18,1280]{1,0:T(8,128)(2,1)S(1)}, bf16[18,1280]{1,0:T(8,128)(2,1)S(1)}, u32[]{:S(2)}, u32[]{:S(2)}) collective-permute-start(bf16[18,1280]{1,0:T(8,128)(2,1)S(1)} %get-tuple-element.31), channel_id=1, source_target_pairs={{0,48},{16,64},{32,80},{48,96},{64,112},{80,0},{96,16},{112,32},{1... | collective-permute-start | bytes 138248 | tf_op jit(solution)/shard_map/ppermute | solution.py:210
  151.8 19.4 %collective-permute-start.12 = (bf16[18,1280]{1,0:T(8,128)(2,1)S(1)}, bf16[18,1280]{1,0:T(8,128)(2,1)S(1)}, u32[]{:S(2)}, u32[]{:S(2)}) collective-permute-start(bf16[18,1280]{1,0:T(8,128)(2,1)S(1)} %get-tuple-element.30), channel_id=1, source_target_pairs={{0,64},{16,80},{32,96},{48,112},{64,0},{80,16},{96,32},{112,48},{1... | collective-permute-start | bytes 138248 | tf_op jit(solution)/shard_map/ppermute | solution.py:210
  157.4 13.9 %collective-permute-start.13 = (bf16[18,1280]{1,0:T(8,128)(2,1)S(1)}, bf16[18,1280]{1,0:T(8,128)(2,1)S(1)}, u32[]{:S(2)}, u32[]{:S(2)}) collective-permute-start(bf16[18,1280]{1,0:T(8,128)(2,1)S(1)} %get-tuple-element.29), channel_id=1, source_target_pairs={{0,80},{16,96},{32,112},{48,0},{64,16},{80,32},{96,48},{112,64},{1... | collective-permute-start | bytes 138248 | tf_op jit(solution)/shard_map/ppermute | solution.py:210
  162.5 8.8 %collective-permute-start.14 = (bf16[18,1280]{1,0:T(8,128)(2,1)S(1)}, bf16[18,1280]{1,0:T(8,128)(2,1)S(1)}, u32[]{:S(2)}, u32[]{:S(2)}) collective-permute-start(bf16[18,1280]{1,0:T(8,128)(2,1)S(1)} %get-tuple-element.28), channel_id=1, source_target_pairs={{0,96},{16,112},{32,0},{48,16},{64,32},{80,48},{96,64},{112,80},{1... | collective-permute-start | bytes 138248 | tf_op jit(solution)/shard_map/ppermute | solution.py:210
  165.4 6.2 %collective-permute-start.15 = (bf16[18,1280]{1,0:T(8,128)(2,1)S(1)}, bf16[18,1280]{1,0:T(8,128)(2,1)S(1)}, u32[]{:S(2)}, u32[]{:S(2)}) collective-permute-start(bf16[18,1280]{1,0:T(8,128)(2,1)S(1)} %get-tuple-element.27), channel_id=1, source_target_pairs={{0,112},{16,0},{32,16},{48,32},{64,48},{80,64},{96,80},{112,96},{1... | collective-permute-start | bytes 138248 | tf_op jit(solution)/shard_map/ppermute | solution.py:210
  167.9 7.3 %collective-permute-start.9 = (bf16[18,1280]{1,0:T(8,128)(2,1)S(1)}, bf16[18,1280]{1,0:T(8,128)(2,1)S(1)}, u32[]{:S(2)}, u32[]{:S(2)}) collective-permute-start(bf16[18,1280]{1,0:T(8,128)(2,1)S(1)} %get-tuple-element.26), channel_id=1, source_target_pairs={{0,16},{16,32},{32,48},{48,64},{64,80},{80,96},{96,112},{112,0},{1... | collective-permute-start | bytes 138248 | tf_op jit(solution)/shard_map/ppermute | solution.py:210
  176.2 16.3 %all-to-all-start.3 = ((f32[8,36,72]{2,1,0:T(8,128)}), f32[8,36,72]{2,1,0:T(8,128)S(1)}, u32[]{:S(2)}, u32[]{:S(2)}) async-start(f32[8,36,72]{2,1,0:T(8,128)} %copy.25), calls=%async_computation.3 | async-start | bytes 327680 | tf_op jit(solution)/shard_map/all_to_all | solution.py:202

commit v2 on v1

--- a/solution.py
+++ b/solution.py
@@ -170,9 +170,23 @@
         to_k.add(head, first, last, dot(slope, block.load(0, at), TN), keep)
 
 
-def part_kernel(mine, send, came, part):
-    total = dot(send[:, HALF:], mine[...], TN) + dot(came[:, HALF:], came[:, :HALF], TN)
-    part[...] = total.astype(jnp.bfloat16).reshape(part.shape)
+def chip_part(mine, send, came):
+    return dot(send[:, HALF:], mine[...], TN) + dot(came[:, HALF:], came[:, :HALF], TN)
+
+
+def part_x_kernel(mine, send, came, part):
+    part[...] = chip_part(mine, send, came).astype(jnp.bfloat16).reshape(part.shape)
+
+
+def part_z_kernel(mine, send, came, part, total, block):
+    side = part.shape[0]
+    rows = total.shape[0] // side**2
+    total[...] = chip_part(mine, send, came)
+    for z in range(side):
+        for x in range(side):
+            start = (x * side + z) * rows
+            block[x * rows : (x + 1) * rows, :] = total[start : start + rows, :]
+        part[z] = block[...].astype(jnp.bfloat16)
 
 
 SM = pl.BlockSpec(memory_space=pltpu.SMEM)
@@ -218,17 +232,19 @@
     return total
 
 
-def part_of(mine, send):
+def part_of(mine, send, z_first):
     width = send.shape[1] - HALF
     side = len(lines(True))
     came = lax.ppermute(send, "seq", [(i, i ^ 1) for i in range(lax.axis_size("seq"))])
+    scratch = [pltpu.VMEM((width, HALF), jnp.float32), pltpu.VMEM((width // side, HALF), jnp.float32)]
     return pl.pallas_call(
-        part_kernel,
+        part_z_kernel if z_first else part_x_kernel,
         in_specs=[VM] * 3,
         out_specs=VM,
         out_shape=shape(side, width // side, HALF),
+        scratch_shapes=scratch if z_first else [],
         cost_estimate=cost(2_000_000_000),
-        name="part",
+        name="part_z" if z_first else "part_x",
     )(mine, send, came)
 
 
@@ -238,8 +254,7 @@
     tokens, width = incoming.shape
     positions = tokens // peers
     side = len(lines(True))
-    x, z = lax.axis_index("dp") // side, lax.axis_index("dp") % side
-    along_x = lambda i, n: (i // side + n) % side * side + i % side
+    z = lax.axis_index("dp") % side
     along_z = lambda i, n: i // side * side + (i % side + n) % side
     blocks = jnp.concatenate([temporal_qkv[0, :, 0], cotangent[0]]).reshape(4, peers, positions, width)
     blocks = jnp.moveaxis(blocks, 1, 0).reshape(peers, 4 * positions, width)
@@ -255,8 +270,7 @@
         cost_estimate=cost(4_000_000_000),
         name="spatial",
     )(live_counts, near(spatial_qkv[0, :, 0]), near(incoming), spatial_gate)
-    part_s = part_of(mine_s, send_s)
-    came_s = shifts(part_s, "dp", x, side, along_x)
+    came_s = shifts(part_of(mine_s, send_s, True), "dp", z, side, along_z)
     mine_t, send_t = pl.pallas_call(
         forward_kernel,
         in_specs=[SM, VM, VM],
@@ -266,7 +280,7 @@
         cost_estimate=cost(4_000_000_000),
         name="forward",
     )(live_counts, arrived, temporal_gate)
-    part_t = part_of(mine_t, send_t)
+    part_t = part_of(mine_t, send_t, False)
     came_t = exchange(part_t, "dp", lines(True))
     grads = pl.pallas_call(
         backward_kernel,
@@ -279,13 +293,14 @@
     )(live_counts, arrived, send_t, temporal_proj)
     came_t, grads = lax.optimization_barrier((came_t, grads))
     home = exchange(grads, "seq")
-    sum_t = summed([came_t[i] for i in range(side)])
-    sums = jnp.concatenate([summed(came_s), sum_t], axis=1).astype(jnp.bfloat16)
-    came = shifts(sums.reshape(side, -1, 2 * HALF), "dp", z, side, along_z)
-    both = summed(came).reshape(-1, 2, HALF)
+    sum_t = summed([came_t[i] for i in range(side)]).astype(jnp.bfloat16)
+    came_t = shifts(sum_t.reshape(side, -1, HALF), "dp", z, side, along_z)
+    sum_s = summed(came_s).astype(jnp.bfloat16)
+    home, sum_s = lax.optimization_barrier((home, sum_s))
+    came_s = exchange(sum_s.reshape(side, -1, HALF), "dp", lines(True))
+    both = jnp.stack([came_s.astype(jnp.float32).sum(axis=0), summed(came_t)], axis=1)
     heads = both[:, :, : HEADS // 2 * HD].reshape(-1, 2, HEADS // 2, HD).transpose(2, 1, 0, 3)
     heads = heads.reshape(HEADS // 2, -1, HD)
-    home, heads = lax.optimization_barrier((home, heads))
     home = jnp.moveaxis(home.reshape(peers, 3, positions, width), 1, 0).reshape(3, 1, tokens, width)
     chips = [[i for i in range(peers) if i % 2 == c] for c in range(2)]
     rows = exchange(heads, "seq", chips).sum(axis=0).reshape(2, -1, HD)

time: 194 us -> 240 us (1.24)
  the two profiles are of different devices: /device:TPU:14 before, /device:TPU:2 now
where the time goes in v2:
time: 240 us; the launch traced here: 239 us
  starting transfers between devices  95.5 us (40%)
  waiting for transfers between devices  63.2 us (26%)
  blocking collectives  38.6 us (16%)
  Pallas kernels  28.6 us (12%)
  local copies, waits for them, and re-layouts  8.25 us (3%)
  other arithmetic  3.91 us (2%)
    ppermute x14, starting transfers between devices, shifts(): lax.ppermute(block, axis, [(i, to(i, step)) for i in range(count)])  62.7 us
    all_to_all x1, blocking collectives, exchange(): lax.all_to_all(blocks, axis, split_axis=0, concat_axis=0, tiled=True, axi...  38.6 us
    all_to_all x4, waiting for transfers between devices, exchange(): lax.all_to_all(blocks, axis, split_axis=0, concat_axis=0, tiled=True, axi...  34.4 us
    all_to_all x4, starting transfers between devices, exchange(): lax.all_to_all(blocks, axis, split_axis=0, concat_axis=0, tiled=True, axi...  27.9 us
    ppermute x14, waiting for transfers between devices, shifts(): lax.ppermute(block, axis, [(i, to(i, step)) for i in range(count)])  25.7 us
    pallas_call x1, Pallas kernels, body(): pl.pallas_call(backward_kernel, in_specs=[SM, VM, VM, VM], out_specs=VM,...  11.4 us
    pallas_call x2, Pallas kernels, part_of(): pl.pallas_call(part_z_kernel if z_first else part_x_kernel, in_specs=[VM]...  6.87 us
    pallas_call x1, Pallas kernels, body(): pl.pallas_call(spatial_kernel, in_specs=[SM, VM, VM, VM], out_specs=[VM]...  5.25 us
  transfers between devices with their start and end apart: 20, of which 10 were waited for; matrix products, arithmetic and copies ran while one was open for 3% of the time, Pallas kernels for 8%

profile of v2, /device:TPU:2, one launch (start us, length us, event | category | flops | bytes accessed | tf_op | source)
XLA Modules:
  0.0 239.2 jit_solution(6795193359104888576)
XLA Ops:
  2.9 38.6 %all_to_all.25.arrived = bf16[16,32,1152]{2,1,0:T(8,128)(2,1)S(1)} all-to-all(bf16[16,32,1152]{2,1,0:T(8,128)(2,1)S(1)} %maximum_bitcast_fusion), channel_id=1, replica_groups=mesh['dp'=64,'seq'=16] {'seq'}, dimensions={0} | all-to-all | bytes 2359296 | tf_op jit(solution)/shard_map/all_to_all | solution.py:216
  41.5 5.2 %forward.1 = (bf16[128,640]{1,0:T(8,128)(2,1)}, bf16[128,1792]{1,0:T(8,128)(2,1)}) custom-call(s32[1,2]{1,0:T(1,128)} %counts.5, bf16[16,32,1152]{2,1,0:T(8,128)(2,1)S(1)} %all_to_all.25.arrived, f32[1,1152]{1,0:T(1,128)} %gate.2), custom_call_target="tpu_custom_call" | custom-call | flops 4000000000 | bytes 4000000 | tf_op jit(solution)/shard_map/forward/pallas_call | solution.py:274
  54.9 12.6 %all-to-all-start.1 = ((bf16[8,144,640]{2,1,0:T(8,128)(2,1)}), bf16[8,144,640]{2,1,0:T(8,128)(2,1)}, u32[]{:S(2)}, u32[]{:S(2)}) async-start(bf16[8,144,640]{2,1,0:T(8,128)(2,1)} %part_x.1), calls=%async_computation.1 | async-start | bytes 2949120 | tf_op jit(solution)/shard_map/all_to_all | solution.py:216
  67.5 11.4 %backward.1 = bf16[16,24,1152]{2,1,0:T(8,128)(2,1)} custom-call(s32[1,2]{1,0:T(1,128)} %counts.5, bf16[16,32,1152]{2,1,0:T(8,128)(2,1)S(1)} %all_to_all.25.arrived, bf16[128,1792]{1,0:T(8,128)(2,1)} %get-tuple-element.12.send, bf16[1152,1152]{1,0:T(8,128)(2,1)} %proj.1), custom_call_target="tpu_custom_call" | custom-call | flops 8000000000 | bytes 4000000 | tf_op jit(solution)/shard_map/backward/pallas_call | solution.py:285
  78.9 26.0 %all-to-all-done.1 = bf16[8,144,640]{2,1,0:T(8,128)(2,1)} async-done(((bf16[8,144,640]{2,1,0:T(8,128)(2,1)}), bf16[8,144,640]{2,1,0:T(8,128)(2,1)}, u32[]{:S(2)}, u32[]{:S(2)}) %all-to-all-start.1) | async-done | bytes 1474592 | tf_op jit(solution)/shard_map/all_to_all | solution.py:216
  104.9 3.6 %all-to-all-start.2 = ((bf16[16,24,1152]{2,1,0:T(8,128)(2,1)}), bf16[16,24,1152]{2,1,0:T(8,128)(2,1)S(1)}, u32[]{:S(2)}, u32[]{:S(2)}) async-start(bf16[16,24,1152]{2,1,0:T(8,128)(2,1)} %backward.1), calls=%async_computation.2 | async-start | bytes 1769472 | tf_op jit(solution)/shard_map/all_to_all | solution.py:216
  108.5 5.2 %spatial.1 = (bf16[128,640]{1,0:T(8,128)(2,1)}, bf16[128,1792]{1,0:T(8,128)(2,1)}) custom-call(s32[1,2]{1,0:T(1,128)} %counts.5, bf16[3,128,1152]{2,1,0:T(8,128)(2,1)S(1)} %bitcast.65, bf16[128,1152]{1,0:T(8,128)(2,1)S(1)} %bitcast.64, f32[1,1152]{1,0:T(1,128)} %gate.3), custom_call_target="tpu_custom_call" | custom-call | flops 4000000000 | bytes 4000000 | tf_op jit(solution)/shard_map/spatial/pallas_call | solution.py:264
  118.5 3.6 %part_z.1 = bf16[8,144,640]{2,1,0:T(8,128)(2,1)} custom-call(bf16[128,640]{1,0:T(8,128)(2,1)} %get-tuple-element.14.mine, bf16[128,1792]{1,0:T(8,128)(2,1)} %get-tuple-element.15.send, bf16[128,1792]{1,0:T(8,128)(2,1)} %copy-done.3), custom_call_target="tpu_custom_call" | custom-call | flops 2000000000 | bytes 4000000 | tf_op jit(solution)/shard_map/part_z/pallas_call | solution.py:240
  126.2 5.6 %collective-permute-start.3 = (bf16[144,640]{1,0:T(8,128)(2,1)S(1)}, bf16[144,640]{1,0:T(8,128)(2,1)S(1)}, u32[]{:S(2)}, u32[]{:S(2)}) collective-permute-start(bf16[144,640]{1,0:T(8,128)(2,1)S(1)} %get-tuple-element.25), channel_id=1, source_target_pairs={{0,32},{16,48},{32,64},{48,80},{64,96},{80,112},{96,0},{112,16},{1... | collective-permute-start | bytes 552968 | tf_op jit(solution)/shard_map/ppermute | solution.py:224
  131.7 10.0 %collective-permute-start.4 = (bf16[144,640]{1,0:T(8,128)(2,1)}, bf16[144,640]{1,0:T(8,128)(2,1)S(1)}, u32[]{:S(2)}, u32[]{:S(2)}) collective-permute-start(bf16[144,640]{1,0:T(8,128)(2,1)} %get-tuple-element.24), channel_id=1, source_target_pairs={{0,48},{16,64},{32,80},{48,96},{64,112},{80,0},{96,16},{112,32},{1... | collective-permute-start | bytes 552968 | tf_op jit(solution)/shard_map/ppermute | solution.py:224
  141.8 3.7 %collective-permute-start.5 = (bf16[144,640]{1,0:T(8,128)(2,1)}, bf16[144,640]{1,0:T(8,128)(2,1)S(1)}, u32[]{:S(2)}, u32[]{:S(2)}) collective-permute-start(bf16[144,640]{1,0:T(8,128)(2,1)} %get-tuple-element.23), channel_id=1, source_target_pairs={{0,64},{16,80},{32,96},{48,112},{64,0},{80,16},{96,32},{112,48},{1... | collective-permute-start | bytes 552968 | tf_op jit(solution)/shard_map/ppermute | solution.py:224
  145.5 6.9 %collective-permute-start.6 = (bf16[144,640]{1,0:T(8,128)(2,1)}, bf16[144,640]{1,0:T(8,128)(2,1)S(1)}, u32[]{:S(2)}, u32[]{:S(2)}) collective-permute-start(bf16[144,640]{1,0:T(8,128)(2,1)} %get-tuple-element.22), channel_id=1, source_target_pairs={{0,80},{16,96},{32,112},{48,0},{64,16},{80,32},{96,48},{112,64},{1... | collective-permute-start | bytes 552968 | tf_op jit(solution)/shard_map/ppermute | solution.py:224
  156.9 5.6 %collective-permute-done.4 = bf16[144,640]{1,0:T(8,128)(2,1)S(1)} collective-permute-done((bf16[144,640]{1,0:T(8,128)(2,1)}, bf16[144,640]{1,0:T(8,128)(2,1)S(1)}, u32[]{:S(2)}, u32[]{:S(2)}) %collective-permute-start.4) | collective-permute-done | bytes 184352 | tf_op jit(solution)/shard_map/ppermute | solution.py:224
  164.3 4.3 %collective-permute-done.6 = bf16[144,640]{1,0:T(8,128)(2,1)S(1)} collective-permute-done((bf16[144,640]{1,0:T(8,128)(2,1)}, bf16[144,640]{1,0:T(8,128)(2,1)S(1)}, u32[]{:S(2)}, u32[]{:S(2)}) %collective-permute-start.6) | collective-permute-done | bytes 184352 | tf_op jit(solution)/shard_map/ppermute | solution.py:224
  168.6 7.2 %collective-permute-done.7 = bf16[144,640]{1,0:T(8,128)(2,1)S(1)} collective-permute-done((bf16[144,640]{1,0:T(8,128)(2,1)S(1)}, bf16[144,640]{1,0:T(8,128)(2,1)S(1)}, u32[]{:S(2)}, u32[]{:S(2)}) %collective-permute-start.7) | collective-permute-done | bytes 184352 | tf_op jit(solution)/shard_map/ppermute | solution.py:224
  181.7 4.8 %all-to-all-start.3 = ((bf16[8,18,640]{2,1,0:T(8,128)(2,1)}), bf16[8,18,640]{2,1,0:T(8,128)(2,1)S(1)}, u32[]{:S(2)}, u32[]{:S(2)}) async-start(bf16[8,18,640]{2,1,0:T(8,128)(2,1)} %reshape.61), calls=%async_computation.3 | async-start | bytes 491520 | tf_op jit(solution)/shard_map/all_to_all | solution.py:216
  186.5 4.0 %collective-permute-start.10 = (bf16[18,640]{1,0:T(8,128)(2,1)S(1)}, bf16[18,640]{1,0:T(8,128)(2,1)S(1)}, u32[]{:S(2)}, u32[]{:S(2)}) collective-permute-start(bf16[18,640]{1,0:T(8,128)(2,1)S(1)} %get-tuple-element.32), channel_id=1, source_target_pairs={{0,32},{16,48},{32,64},{48,80},{64,96},{80,112},{96,0},{112,16},{1... | collective-permute-start | bytes 69128 | tf_op jit(solution)/shard_map/ppermute | solution.py:224
  190.5 5.9 %collective-permute-start.11 = (bf16[18,640]{1,0:T(8,128)(2,1)S(1)}, bf16[18,640]{1,0:T(8,128)(2,1)S(1)}, u32[]{:S(2)}, u32[]{:S(2)}) collective-permute-start(bf16[18,640]{1,0:T(8,128)(2,1)S(1)} %get-tuple-element.31), channel_id=1, source_target_pairs={{0,48},{16,64},{32,80},{48,96},{64,112},{80,0},{96,16},{112,32},{1... | collective-permute-start | bytes 69128 | tf_op jit(solution)/shard_map/ppermute | solution.py:224
  196.4 3.8 %collective-permute-start.12 = (bf16[18,640]{1,0:T(8,128)(2,1)S(1)}, bf16[18,640]{1,0:T(8,128)(2,1)S(1)}, u32[]{:S(2)}, u32[]{:S(2)}) collective-permute-start(bf16[18,640]{1,0:T(8,128)(2,1)S(1)} %get-tuple-element.30), channel_id=1, source_target_pairs={{0,64},{16,80},{32,96},{48,112},{64,0},{80,16},{96,32},{112,48},{1... | collective-permute-start | bytes 69128 | tf_op jit(solution)/shard_map/ppermute | solution.py:224
  200.3 5.1 %collective-permute-start.13 = (bf16[18,640]{1,0:T(8,128)(2,1)S(1)}, bf16[18,640]{1,0:T(8,128)(2,1)S(1)}, u32[]{:S(2)}, u32[]{:S(2)}) collective-permute-start(bf16[18,640]{1,0:T(8,128)(2,1)S(1)} %get-tuple-element.29), channel_id=1, source_target_pairs={{0,80},{16,96},{32,112},{48,0},{64,16},{80,32},{96,48},{112,64},{1... | collective-permute-start | bytes 69128 | tf_op jit(solution)/shard_map/ppermute | solution.py:224
  205.3 5.5 %collective-permute-start.14 = (bf16[18,640]{1,0:T(8,128)(2,1)S(1)}, bf16[18,640]{1,0:T(8,128)(2,1)S(1)}, u32[]{:S(2)}, u32[]{:S(2)}) collective-permute-start(bf16[18,640]{1,0:T(8,128)(2,1)S(1)} %get-tuple-element.28), channel_id=1, source_target_pairs={{0,96},{16,112},{32,0},{48,16},{64,32},{80,48},{96,64},{112,80},{1... | collective-permute-start | bytes 69128 | tf_op jit(solution)/shard_map/ppermute | solution.py:224
  216.8 4.4 %collective-permute-done.9 = bf16[18,640]{1,0:T(8,128)(2,1)S(1)} collective-permute-done((bf16[18,640]{1,0:T(8,128)(2,1)S(1)}, bf16[18,640]{1,0:T(8,128)(2,1)S(1)}, u32[]{:S(2)}, u32[]{:S(2)}) %collective-permute-start.9) | collective-permute-done | bytes 23072 | tf_op jit(solution)/shard_map/ppermute | solution.py:224
  222.3 6.9 %all-to-all-start.4 = ((f32[8,36,72]{2,1,0:T(8,128)}), f32[8,36,72]{2,1,0:T(8,128)S(1)}, u32[]{:S(2)}, u32[]{:S(2)}) async-start(f32[8,36,72]{2,1,0:T(8,128)} %copy.27), calls=%async_computation.4 | async-start | bytes 327680 | tf_op jit(solution)/shard_map/all_to_all | solution.py:216
  230.1 8.4 %all-to-all-done.4 = f32[8,36,72]{2,1,0:T(8,128)S(1)} async-done(((f32[8,36,72]{2,1,0:T(8,128)}), f32[8,36,72]{2,1,0:T(8,128)S(1)}, u32[]{:S(2)}, u32[]{:S(2)}) %all-to-all-start.4) | async-done | bytes 82976 | tf_op jit(solution)/shard_map/all_to_all | solution.py:216
  (49 shorter events, 39.7 us)
Async XLA Ops:
  0.6 1.2 copy-start
  46.7 4.2 %collective-permute-start = (bf16[128,1792]{1,0:T(8,128)(2,1)}, bf16[128,1792]{1,0:T(8,128)(2,1)S(1)}, u32[]{:S(2)}, u32[]{:S(2)}) collective-permute-start(bf16[128,1792]{1,0:T(8,128)(2,1)} %get-tuple-element.12.send), channel_id=1, source_target_pairs={{0,1},{1,0},{2,3},{3,2},{4,5},{5,4},{6,7},{7,6},{8,9},{9,8},{10,11... | collective-permute-start | bytes 1376264 | tf_op jit(solution)/shard_map/ppermute | solution.py:238
  50.9 0.8 copy-start.4
  54.9 50.0 %all-to-all-start.1 = ((bf16[8,144,640]{2,1,0:T(8,128)(2,1)}), bf16[8,144,640]{2,1,0:T(8,128)(2,1)}, u32[]{:S(2)}, u32[]{:S(2)}) async-start(bf16[8,144,640]{2,1,0:T(8,128)(2,1)} %part_x.1), calls=%async_computation.1 | async-start | bytes 2949120 | tf_op jit(solution)/shard_map/all_to_all | solution.py:216
  78.9 29.6 %copy-start.1 = (bf16[1,1,128,1152]{3,2,1,0:T(8,128)(2,1)S(1)}, bf16[1,1,128,1152]{3,2,1,0:T(8,128)(2,1)}, u32[]{:S(2)}) copy-start(bf16[1,1,128,1152]{3,2,1,0:T(8,128)(2,1)} %param.9) | copy-start | bytes 884740
  78.9 29.6 %copy-start.2 = (bf16[1,3,1,128,1152]{4,3,2,1,0:T(8,128)(2,1)S(1)}, bf16[1,3,1,128,1152]{4,3,2,1,0:T(8,128)(2,1)}, u32[]{:S(2)}) copy-start(bf16[1,3,1,128,1152]{4,3,2,1,0:T(8,128)(2,1)} %param.7) | copy-start | bytes 2654212
  104.9 76.1 %all-to-all-start.2 = ((bf16[16,24,1152]{2,1,0:T(8,128)(2,1)}), bf16[16,24,1152]{2,1,0:T(8,128)(2,1)S(1)}, u32[]{:S(2)}, u32[]{:S(2)}) async-start(bf16[16,24,1152]{2,1,0:T(8,128)(2,1)} %backward.1), calls=%async_computation.2 | async-start | bytes 1769472 | tf_op jit(solution)/shard_map/all_to_all | solution.py:216
  113.8 3.9 %collective-permute-start.1 = (bf16[128,1792]{1,0:T(8,128)(2,1)}, bf16[128,1792]{1,0:T(8,128)(2,1)S(1)}, u32[]{:S(2)}, u32[]{:S(2)}) collective-permute-start(bf16[128,1792]{1,0:T(8,128)(2,1)} %get-tuple-element.15.send), channel_id=1, source_target_pairs={{0,1},{1,0},{2,3},{3,2},{4,5},{5,4},{6,7},{7,6},{8,9},{9,8},{10,11... | collective-permute-start | bytes 1376264 | tf_op jit(solution)/shard_map/ppermute | solution.py:238
  124.2 28.2 %collective-permute-start.2 = (bf16[144,640]{1,0:T(8,128)(2,1)S(1)}, bf16[144,640]{1,0:T(8,128)(2,1)S(1)}, u32[]{:S(2)}, u32[]{:S(2)}) collective-permute-start(bf16[144,640]{1,0:T(8,128)(2,1)S(1)} %get-tuple-element.19), channel_id=1, source_target_pairs={{0,16},{16,32},{32,48},{48,64},{64,80},{80,96},{96,112},{112,0},{1... | collective-permute-start | bytes 552968 | tf_op jit(solution)/shard_map/ppermute | solution.py:224
  126.2 28.2 %collective-permute-start.3 = (bf16[144,640]{1,0:T(8,128)(2,1)S(1)}, bf16[144,640]{1,0:T(8,128)(2,1)S(1)}, u32[]{:S(2)}, u32[]{:S(2)}) collective-permute-start(bf16[144,640]{1,0:T(8,128)(2,1)S(1)} %get-tuple-element.25), channel_id=1, source_target_pairs={{0,32},{16,48},{32,64},{48,80},{64,96},{80,112},{96,0},{112,16},{1... | collective-permute-start | bytes 552968 | tf_op jit(solution)/shard_map/ppermute | solution.py:224
  131.7 30.8 %collective-permute-start.4 = (bf16[144,640]{1,0:T(8,128)(2,1)}, bf16[144,640]{1,0:T(8,128)(2,1)S(1)}, u32[]{:S(2)}, u32[]{:S(2)}) collective-permute-start(bf16[144,640]{1,0:T(8,128)(2,1)} %get-tuple-element.24), channel_id=1, source_target_pairs={{0,48},{16,64},{32,80},{48,96},{64,112},{80,0},{96,16},{112,32},{1... | collective-permute-start | bytes 552968 | tf_op jit(solution)/shard_map/ppermute | solution.py:224
  141.8 22.5 %collective-permute-start.5 = (bf16[144,640]{1,0:T(8,128)(2,1)}, bf16[144,640]{1,0:T(8,128)(2,1)S(1)}, u32[]{:S(2)}, u32[]{:S(2)}) collective-permute-start(bf16[144,640]{1,0:T(8,128)(2,1)} %get-tuple-element.23), channel_id=1, source_target_pairs={{0,64},{16,80},{32,96},{48,112},{64,0},{80,16},{96,32},{112,48},{1... | collective-permute-start | bytes 552968 | tf_op jit(solution)/shard_map/ppermute | solution.py:224
  145.5 23.1 %collective-permute-start.6 = (bf16[144,640]{1,0:T(8,128)(2,1)}, bf16[144,640]{1,0:T(8,128)(2,1)S(1)}, u32[]{:S(2)}, u32[]{:S(2)}) collective-permute-start(bf16[144,640]{1,0:T(8,128)(2,1)} %get-tuple-element.22), channel_id=1, source_target_pairs={{0,80},{16,96},{32,112},{48,0},{64,16},{80,32},{96,48},{112,64},{1... | collective-permute-start | bytes 552968 | tf_op jit(solution)/shard_map/ppermute | solution.py:224
  152.5 23.3 %collective-permute-start.7 = (bf16[144,640]{1,0:T(8,128)(2,1)S(1)}, bf16[144,640]{1,0:T(8,128)(2,1)S(1)}, u32[]{:S(2)}, u32[]{:S(2)}) collective-permute-start(bf16[144,640]{1,0:T(8,128)(2,1)S(1)} %get-tuple-element.21), channel_id=1, source_target_pairs={{0,96},{16,112},{32,0},{48,16},{64,32},{80,48},{96,64},{112,80},{1... | collective-permute-start | bytes 552968 | tf_op jit(solution)/shard_map/ppermute | solution.py:224
  154.4 23.8 %collective-permute-start.8 = (bf16[144,640]{1,0:T(8,128)(2,1)S(1)}, bf16[144,640]{1,0:T(8,128)(2,1)S(1)}, u32[]{:S(2)}, u32[]{:S(2)}) collective-permute-start(bf16[144,640]{1,0:T(8,128)(2,1)S(1)} %get-tuple-element.20), channel_id=1, source_target_pairs={{0,112},{16,0},{32,16},{48,32},{64,48},{80,64},{96,80},{112,96},{1... | collective-permute-start | bytes 552968 | tf_op jit(solution)/shard_map/ppermute | solution.py:224
  181.7 39.5 %all-to-all-start.3 = ((bf16[8,18,640]{2,1,0:T(8,128)(2,1)}), bf16[8,18,640]{2,1,0:T(8,128)(2,1)S(1)}, u32[]{:S(2)}, u32[]{:S(2)}) async-start(bf16[8,18,640]{2,1,0:T(8,128)(2,1)} %reshape.61), calls=%async_computation.3 | async-start | bytes 491520 | tf_op jit(solution)/shard_map/all_to_all | solution.py:216
  186.5 24.3 %collective-permute-start.10 = (bf16[18,640]{1,0:T(8,128)(2,1)S(1)}, bf16[18,640]{1,0:T(8,128)(2,1)S(1)}, u32[]{:S(2)}, u32[]{:S(2)}) collective-permute-start(bf16[18,640]{1,0:T(8,128)(2,1)S(1)} %get-tuple-element.32), channel_id=1, source_target_pairs={{0,32},{16,48},{32,64},{48,80},{64,96},{80,112},{96,0},{112,16},{1... | collective-permute-start | bytes 69128 | tf_op jit(solution)/shard_map/ppermute | solution.py:224
  190.5 23.7 %collective-permute-start.11 = (bf16[18,640]{1,0:T(8,128)(2,1)S(1)}, bf16[18,640]{1,0:T(8,128)(2,1)S(1)}, u32[]{:S(2)}, u32[]{:S(2)}) collective-permute-start(bf16[18,640]{1,0:T(8,128)(2,1)S(1)} %get-tuple-element.31), channel_id=1, source_target_pairs={{0,48},{16,64},{32,80},{48,96},{64,112},{80,0},{96,16},{112,32},{1... | collective-permute-start | bytes 69128 | tf_op jit(solution)/shard_map/ppermute | solution.py:224
  196.4 20.3 %collective-permute-start.12 = (bf16[18,640]{1,0:T(8,128)(2,1)S(1)}, bf16[18,640]{1,0:T(8,128)(2,1)S(1)}, u32[]{:S(2)}, u32[]{:S(2)}) collective-permute-start(bf16[18,640]{1,0:T(8,128)(2,1)S(1)} %get-tuple-element.30), channel_id=1, source_target_pairs={{0,64},{16,80},{32,96},{48,112},{64,0},{80,16},{96,32},{112,48},{1... | collective-permute-start | bytes 69128 | tf_op jit(solution)/shard_map/ppermute | solution.py:224
  200.3 16.5 %collective-permute-start.13 = (bf16[18,640]{1,0:T(8,128)(2,1)S(1)}, bf16[18,640]{1,0:T(8,128)(2,1)S(1)}, u32[]{:S(2)}, u32[]{:S(2)}) collective-permute-start(bf16[18,640]{1,0:T(8,128)(2,1)S(1)} %get-tuple-element.29), channel_id=1, source_target_pairs={{0,80},{16,96},{32,112},{48,0},{64,16},{80,32},{96,48},{112,64},{1... | collective-permute-start | bytes 69128 | tf_op jit(solution)/shard_map/ppermute | solution.py:224
  205.3 11.4 %collective-permute-start.14 = (bf16[18,640]{1,0:T(8,128)(2,1)S(1)}, bf16[18,640]{1,0:T(8,128)(2,1)S(1)}, u32[]{:S(2)}, u32[]{:S(2)}) collective-permute-start(bf16[18,640]{1,0:T(8,128)(2,1)S(1)} %get-tuple-element.28), channel_id=1, source_target_pairs={{0,96},{16,112},{32,0},{48,16},{64,32},{80,48},{96,64},{112,80},{1... | collective-permute-start | bytes 69128 | tf_op jit(solution)/shard_map/ppermute | solution.py:224
  210.9 5.9 %collective-permute-start.15 = (bf16[18,640]{1,0:T(8,128)(2,1)S(1)}, bf16[18,640]{1,0:T(8,128)(2,1)S(1)}, u32[]{:S(2)}, u32[]{:S(2)}) collective-permute-start(bf16[18,640]{1,0:T(8,128)(2,1)S(1)} %get-tuple-element.27), channel_id=1, source_target_pairs={{0,112},{16,0},{32,16},{48,32},{64,48},{80,64},{96,80},{112,96},{1... | collective-permute-start | bytes 69128 | tf_op jit(solution)/shard_map/ppermute | solution.py:224
  214.2 7.0 %collective-permute-start.9 = (bf16[18,640]{1,0:T(8,128)(2,1)S(1)}, bf16[18,640]{1,0:T(8,128)(2,1)S(1)}, u32[]{:S(2)}, u32[]{:S(2)}) collective-permute-start(bf16[18,640]{1,0:T(8,128)(2,1)S(1)} %get-tuple-element.26), channel_id=1, source_target_pairs={{0,16},{16,32},{32,48},{48,64},{64,80},{80,96},{96,112},{112,0},{1... | collective-permute-start | bytes 69128 | tf_op jit(solution)/shard_map/ppermute | solution.py:224
  222.3 16.3 %all-to-all-start.4 = ((f32[8,36,72]{2,1,0:T(8,128)}), f32[8,36,72]{2,1,0:T(8,128)S(1)}, u32[]{:S(2)}, u32[]{:S(2)}) async-start(f32[8,36,72]{2,1,0:T(8,128)} %copy.27), calls=%async_computation.4 | async-start | bytes 327680 | tf_op jit(solution)/shard_map/all_to_all | solution.py:216
  (1 other events, 0.8 us)

commit v3 on v2

--- a/solution.py
+++ b/solution.py
@@ -254,7 +254,8 @@
     tokens, width = incoming.shape
     positions = tokens // peers
     side = len(lines(True))
-    z = lax.axis_index("dp") % side
+    x, z = lax.axis_index("dp") // side, lax.axis_index("dp") % side
+    along_x = lambda i, n: (i // side + n) % side * side + i % side
     along_z = lambda i, n: i // side * side + (i % side + n) % side
     blocks = jnp.concatenate([temporal_qkv[0, :, 0], cotangent[0]]).reshape(4, peers, positions, width)
     blocks = jnp.moveaxis(blocks, 1, 0).reshape(peers, 4 * positions, width)
@@ -292,15 +293,16 @@
         name="backward",
     )(live_counts, arrived, send_t, temporal_proj)
     came_t, grads = lax.optimization_barrier((came_t, grads))
+    sum_t = summed([came_t[i] for i in range(side)]).astype(jnp.bfloat16)
+    came_t = exchange(sum_t.reshape(side, -1, HALF), "dp", lines(False))
+    sum_s = summed(came_s).astype(jnp.bfloat16)
+    came_t, grads, sum_s = lax.optimization_barrier((came_t, grads, sum_s))
     home = exchange(grads, "seq")
-    sum_t = summed([came_t[i] for i in range(side)]).astype(jnp.bfloat16)
-    came_t = shifts(sum_t.reshape(side, -1, HALF), "dp", z, side, along_z)
-    sum_s = summed(came_s).astype(jnp.bfloat16)
-    home, sum_s = lax.optimization_barrier((home, sum_s))
-    came_s = exchange(sum_s.reshape(side, -1, HALF), "dp", lines(True))
-    both = jnp.stack([came_s.astype(jnp.float32).sum(axis=0), summed(came_t)], axis=1)
+    came_s = shifts(sum_s.reshape(side, -1, HALF), "dp", x, side, along_x)
+    both = jnp.stack([summed(came_s), came_t.astype(jnp.float32).sum(axis=0)], axis=1)
     heads = both[:, :, : HEADS // 2 * HD].reshape(-1, 2, HEADS // 2, HD).transpose(2, 1, 0, 3)
     heads = heads.reshape(HEADS // 2, -1, HD)
+    home, heads = lax.optimization_barrier((home, heads))
     home = jnp.moveaxis(home.reshape(peers, 3, positions, width), 1, 0).reshape(3, 1, tokens, width)
     chips = [[i for i in range(peers) if i % 2 == c] for c in range(2)]
     rows = exchange(heads, "seq", chips).sum(axis=0).reshape(2, -1, HD)

time: 240 us -> 201 us (0.84)
  the two profiles are of different devices: /device:TPU:2 before, /device:TPU:16 now
where the time goes in v3:
time: 201 us; the launch traced here: 200 us
  starting transfers between devices  90.1 us (45%)
  blocking collectives  45.2 us (22%)
  Pallas kernels  28.6 us (14%)
  waiting for transfers between devices  22.6 us (11%)
  local copies, waits for them, and re-layouts  8.37 us (4%)
  other arithmetic  3.9 us (2%)
    ppermute x14, starting transfers between devices, shifts(): lax.ppermute(block, axis, [(i, to(i, step)) for i in range(count)])  62.4 us
    all_to_all x1, blocking collectives, exchange(): lax.all_to_all(blocks, axis, split_axis=0, concat_axis=0, tiled=True, axi...  45.2 us
    all_to_all x4, starting transfers between devices, exchange(): lax.all_to_all(blocks, axis, split_axis=0, concat_axis=0, tiled=True, axi...  22.8 us
    pallas_call x1, Pallas kernels, body(): pl.pallas_call(backward_kernel, in_specs=[SM, VM, VM, VM], out_specs=VM,...  11.4 us
    all_to_all x4, waiting for transfers between devices, exchange(): lax.all_to_all(blocks, axis, split_axis=0, concat_axis=0, tiled=True, axi...  10.6 us
    ppermute x14, waiting for transfers between devices, shifts(): lax.ppermute(block, axis, [(i, to(i, step)) for i in range(count)])  8.94 us
    pallas_call x2, Pallas kernels, part_of(): pl.pallas_call(part_z_kernel if z_first else part_x_kernel, in_specs=[VM]...  6.9 us
    pallas_call x1, Pallas kernels, body(): pl.pallas_call(spatial_kernel, in_specs=[SM, VM, VM, VM], out_specs=[VM]...  5.2 us
  transfers between devices with their start and end apart: 20, of which 6 were waited for; matrix products, arithmetic and copies ran while one was open for 4% of the time, Pallas kernels for 10%

profile of v3, /device:TPU:16, one launch (start us, length us, event | category | flops | bytes accessed | tf_op | source)
XLA Modules:
  0.0 199.9 jit_solution(13255043363533055512)
XLA Ops:
  2.9 45.2 %all_to_all.25.arrived = bf16[16,32,1152]{2,1,0:T(8,128)(2,1)S(1)} all-to-all(bf16[16,32,1152]{2,1,0:T(8,128)(2,1)S(1)} %maximum_bitcast_fusion), channel_id=1, replica_groups=mesh['dp'=64,'seq'=16] {'seq'}, dimensions={0} | all-to-all | bytes 2359296 | tf_op jit(solution)/shard_map/all_to_all | solution.py:216
  48.1 5.2 %forward.1 = (bf16[128,640]{1,0:T(8,128)(2,1)}, bf16[128,1792]{1,0:T(8,128)(2,1)}) custom-call(s32[1,2]{1,0:T(1,128)} %counts.5, bf16[16,32,1152]{2,1,0:T(8,128)(2,1)S(1)} %all_to_all.25.arrived, f32[1,1152]{1,0:T(1,128)} %gate.2), custom_call_target="tpu_custom_call" | custom-call | flops 4000000000 | bytes 4000000 | tf_op jit(solution)/shard_map/forward/pallas_call | solution.py:275
  58.2 3.3 %part_x.1 = bf16[8,144,640]{2,1,0:T(8,128)(2,1)} custom-call(bf16[128,640]{1,0:T(8,128)(2,1)} %get-tuple-element.14.mine, bf16[128,1792]{1,0:T(8,128)(2,1)} %get-tuple-element.15.send, bf16[128,1792]{1,0:T(8,128)(2,1)} %copy-done.4), custom_call_target="tpu_custom_call" | custom-call | flops 2000000000 | bytes 4000000 | tf_op jit(solution)/shard_map/part_x/pallas_call | solution.py:240
  61.6 4.4 %all-to-all-start.1 = ((bf16[8,144,640]{2,1,0:T(8,128)(2,1)}), bf16[8,144,640]{2,1,0:T(8,128)(2,1)}, u32[]{:S(2)}, u32[]{:S(2)}) async-start(bf16[8,144,640]{2,1,0:T(8,128)(2,1)} %part_x.1), calls=%async_computation.1 | async-start | bytes 2949120 | tf_op jit(solution)/shard_map/all_to_all | solution.py:216
  66.0 5.2 %spatial.1 = (bf16[128,640]{1,0:T(8,128)(2,1)}, bf16[128,1792]{1,0:T(8,128)(2,1)}) custom-call(s32[1,2]{1,0:T(1,128)} %counts.5, bf16[3,128,1152]{2,1,0:T(8,128)(2,1)S(1)} %bitcast.65, bf16[128,1152]{1,0:T(8,128)(2,1)S(1)} %bitcast.64, f32[1,1152]{1,0:T(1,128)} %gate.3), custom_call_target="tpu_custom_call" | custom-call | flops 4000000000 | bytes 4000000 | tf_op jit(solution)/shard_map/spatial/pallas_call | solution.py:265
  75.9 3.6 %part_z.1 = bf16[8,144,640]{2,1,0:T(8,128)(2,1)} custom-call(bf16[128,640]{1,0:T(8,128)(2,1)} %get-tuple-element.18.mine, bf16[128,1792]{1,0:T(8,128)(2,1)} %get-tuple-element.19.send, bf16[128,1792]{1,0:T(8,128)(2,1)} %copy-done.3), custom_call_target="tpu_custom_call" | custom-call | flops 2000000000 | bytes 4000000 | tf_op jit(solution)/shard_map/part_z/pallas_call | solution.py:240
  81.8 12.0 %collective-permute-start.8 = (bf16[144,640]{1,0:T(8,128)(2,1)}, bf16[144,640]{1,0:T(8,128)(2,1)S(1)}, u32[]{:S(2)}, u32[]{:S(2)}) collective-permute-start(bf16[144,640]{1,0:T(8,128)(2,1)} %get-tuple-element.26), channel_id=1, source_target_pairs={{0,112},{16,0},{32,16},{48,32},{64,48},{80,64},{96,80},{112,96},{1... | collective-permute-start | bytes 552968 | tf_op jit(solution)/shard_map/ppermute | solution.py:224
  97.7 7.8 %collective-permute-start.5 = (bf16[144,640]{1,0:T(8,128)(2,1)}, bf16[144,640]{1,0:T(8,128)(2,1)S(1)}, u32[]{:S(2)}, u32[]{:S(2)}) collective-permute-start(bf16[144,640]{1,0:T(8,128)(2,1)} %get-tuple-element.29), channel_id=1, source_target_pairs={{0,64},{16,80},{32,96},{48,112},{64,0},{80,16},{96,32},{112,48},{1... | collective-permute-start | bytes 552968 | tf_op jit(solution)/shard_map/ppermute | solution.py:224
  107.6 11.4 %backward.1 = bf16[16,24,1152]{2,1,0:T(8,128)(2,1)} custom-call(s32[1,2]{1,0:T(1,128)} %counts.5, bf16[16,32,1152]{2,1,0:T(8,128)(2,1)S(1)} %all_to_all.25.arrived, bf16[128,1792]{1,0:T(8,128)(2,1)} %get-tuple-element.15.send, bf16[1152,1152]{1,0:T(8,128)(2,1)} %proj.1), custom_call_target="tpu_custom_call" | custom-call | flops 8000000000 | bytes 4000000 | tf_op jit(solution)/shard_map/backward/pallas_call | solution.py:286
  119.0 3.9 %collective-permute-start.3 = (bf16[144,640]{1,0:T(8,128)(2,1)S(1)}, bf16[144,640]{1,0:T(8,128)(2,1)S(1)}, u32[]{:S(2)}, u32[]{:S(2)}) collective-permute-start(bf16[144,640]{1,0:T(8,128)(2,1)S(1)} %get-tuple-element.31), channel_id=1, source_target_pairs={{0,32},{16,48},{32,64},{48,80},{64,96},{80,112},{96,0},{112,16},{1... | collective-permute-start | bytes 552968 | tf_op jit(solution)/shard_map/ppermute | solution.py:224
  123.0 3.4 %collective-permute-start.2 = (bf16[144,640]{1,0:T(8,128)(2,1)S(1)}, bf16[144,640]{1,0:T(8,128)(2,1)S(1)}, u32[]{:S(2)}, u32[]{:S(2)}) collective-permute-start(bf16[144,640]{1,0:T(8,128)(2,1)S(1)} %get-tuple-element.25), channel_id=1, source_target_pairs={{0,16},{16,32},{32,48},{48,64},{64,80},{80,96},{96,112},{112,0},{1... | collective-permute-start | bytes 552968 | tf_op jit(solution)/shard_map/ppermute | solution.py:224
  128.7 6.3 %all-to-all-start.2 = ((bf16[8,18,640]{2,1,0:T(8,128)(2,1)}), bf16[8,18,640]{2,1,0:T(8,128)(2,1)S(1)}, u32[]{:S(2)}, u32[]{:S(2)}) async-start(bf16[8,18,640]{2,1,0:T(8,128)(2,1)} %reshape.74), calls=%async_computation.2 | async-start | bytes 491520 | tf_op jit(solution)/shard_map/all_to_all | solution.py:216
  135.0 5.4 %collective-permute-done.2 = bf16[144,640]{1,0:T(8,128)(2,1)S(1)} collective-permute-done((bf16[144,640]{1,0:T(8,128)(2,1)S(1)}, bf16[144,640]{1,0:T(8,128)(2,1)S(1)}, u32[]{:S(2)}, u32[]{:S(2)}) %collective-permute-start.2) | collective-permute-done | bytes 184352 | tf_op jit(solution)/shard_map/ppermute | solution.py:224
  141.6 3.6 %all-to-all-done.2 = bf16[8,18,640]{2,1,0:T(8,128)(2,1)S(1)} async-done(((bf16[8,18,640]{2,1,0:T(8,128)(2,1)}), bf16[8,18,640]{2,1,0:T(8,128)(2,1)S(1)}, u32[]{:S(2)}, u32[]{:S(2)}) %all-to-all-start.2) | async-done | bytes 184352 | tf_op jit(solution)/shard_map/all_to_all | solution.py:216
  145.1 4.9 %all-to-all-start.3 = ((bf16[16,24,1152]{2,1,0:T(8,128)(2,1)}), bf16[16,24,1152]{2,1,0:T(8,128)(2,1)S(1)}, u32[]{:S(2)}, u32[]{:S(2)}) async-start(bf16[16,24,1152]{2,1,0:T(8,128)(2,1)} %backward.1), calls=%async_computation.3 | async-start | bytes 1769472 | tf_op jit(solution)/shard_map/all_to_all | solution.py:216
  150.1 5.1 %collective-permute-start.15 = (bf16[18,640]{1,0:T(8,128)(2,1)S(1)}, bf16[18,640]{1,0:T(8,128)(2,1)S(1)}, u32[]{:S(2)}, u32[]{:S(2)}) collective-permute-start(bf16[18,640]{1,0:T(8,128)(2,1)S(1)} %get-tuple-element.33), channel_id=1, source_target_pairs={{0,896},{16,912},{32,928},{48,944},{64,960},{80,976},{96,992},{112... | collective-permute-start | bytes 69128 | tf_op jit(solution)/shard_map/ppermute | solution.py:224
  155.3 4.3 %collective-permute-start.14 = (bf16[18,640]{1,0:T(8,128)(2,1)S(1)}, bf16[18,640]{1,0:T(8,128)(2,1)S(1)}, u32[]{:S(2)}, u32[]{:S(2)}) collective-permute-start(bf16[18,640]{1,0:T(8,128)(2,1)S(1)} %get-tuple-element.34), channel_id=1, source_target_pairs={{0,768},{16,784},{32,800},{48,816},{64,832},{80,848},{96,864},{112... | collective-permute-start | bytes 69128 | tf_op jit(solution)/shard_map/ppermute | solution.py:224
  159.6 3.4 %collective-permute-start.13 = (bf16[18,640]{1,0:T(8,128)(2,1)S(1)}, bf16[18,640]{1,0:T(8,128)(2,1)S(1)}, u32[]{:S(2)}, u32[]{:S(2)}) collective-permute-start(bf16[18,640]{1,0:T(8,128)(2,1)S(1)} %get-tuple-element.35), channel_id=1, source_target_pairs={{0,640},{16,656},{32,672},{48,688},{64,704},{80,720},{96,736},{112... | collective-permute-start | bytes 69128 | tf_op jit(solution)/shard_map/ppermute | solution.py:224
  162.9 5.5 %collective-permute-start.12 = (bf16[18,640]{1,0:T(8,128)(2,1)S(1)}, bf16[18,640]{1,0:T(8,128)(2,1)S(1)}, u32[]{:S(2)}, u32[]{:S(2)}) collective-permute-start(bf16[18,640]{1,0:T(8,128)(2,1)S(1)} %get-tuple-element.36), channel_id=1, source_target_pairs={{0,512},{16,528},{32,544},{48,560},{64,576},{80,592},{96,608},{112... | collective-permute-start | bytes 69128 | tf_op jit(solution)/shard_map/ppermute | solution.py:224
  170.6 5.5 %collective-permute-start.10 = (bf16[18,640]{1,0:T(8,128)(2,1)S(1)}, bf16[18,640]{1,0:T(8,128)(2,1)S(1)}, u32[]{:S(2)}, u32[]{:S(2)}) collective-permute-start(bf16[18,640]{1,0:T(8,128)(2,1)S(1)} %get-tuple-element.38), channel_id=1, source_target_pairs={{0,256},{16,272},{32,288},{48,304},{64,320},{80,336},{96,352},{112... | collective-permute-start | bytes 69128 | tf_op jit(solution)/shard_map/ppermute | solution.py:224
  176.1 3.4 %collective-permute-start.9 = (bf16[18,640]{1,0:T(8,128)(2,1)S(1)}, bf16[18,640]{1,0:T(8,128)(2,1)S(1)}, u32[]{:S(2)}, u32[]{:S(2)}) collective-permute-start(bf16[18,640]{1,0:T(8,128)(2,1)S(1)} %get-tuple-element.32), channel_id=1, source_target_pairs={{0,128},{16,144},{32,160},{48,176},{64,192},{80,208},{96,224},{112... | collective-permute-start | bytes 69128 | tf_op jit(solution)/shard_map/ppermute | solution.py:224
  179.6 3.5 %collective-permute-done.9 = bf16[18,640]{1,0:T(8,128)(2,1)S(1)} collective-permute-done((bf16[18,640]{1,0:T(8,128)(2,1)S(1)}, bf16[18,640]{1,0:T(8,128)(2,1)S(1)}, u32[]{:S(2)}, u32[]{:S(2)}) %collective-permute-start.9) | collective-permute-done | bytes 23072 | tf_op jit(solution)/shard_map/ppermute | solution.py:224
  184.1 7.2 %all-to-all-start.4 = ((f32[8,36,72]{2,1,0:T(8,128)}), f32[8,36,72]{2,1,0:T(8,128)S(1)}, u32[]{:S(2)}, u32[]{:S(2)}) async-start(f32[8,36,72]{2,1,0:T(8,128)} %copy.27), calls=%async_computation.4 | async-start | bytes 327680 | tf_op jit(solution)/shard_map/all_to_all | solution.py:216
  192.3 7.0 %all-to-all-done.4 = f32[8,36,72]{2,1,0:T(8,128)S(1)} async-done(((f32[8,36,72]{2,1,0:T(8,128)}), f32[8,36,72]{2,1,0:T(8,128)S(1)}, u32[]{:S(2)}, u32[]{:S(2)}) %all-to-all-start.4) | async-done | bytes 82976 | tf_op jit(solution)/shard_map/all_to_all | solution.py:216
  (49 shorter events, 28.4 us)
Async XLA Ops:
  0.6 1.2 copy-start
  53.2 4.2 %collective-permute-start = (bf16[128,1792]{1,0:T(8,128)(2,1)}, bf16[128,1792]{1,0:T(8,128)(2,1)S(1)}, u32[]{:S(2)}, u32[]{:S(2)}) collective-permute-start(bf16[128,1792]{1,0:T(8,128)(2,1)} %get-tuple-element.15.send), channel_id=1, source_target_pairs={{0,1},{1,0},{2,3},{3,2},{4,5},{5,4},{6,7},{7,6},{8,9},{9,8},{10,11... | collective-permute-start | bytes 1376264 | tf_op jit(solution)/shard_map/ppermute | solution.py:238
  61.6 4.4 %copy-start.1 = (bf16[1,1,128,1152]{3,2,1,0:T(8,128)(2,1)S(1)}, bf16[1,1,128,1152]{3,2,1,0:T(8,128)(2,1)}, u32[]{:S(2)}) copy-start(bf16[1,1,128,1152]{3,2,1,0:T(8,128)(2,1)} %param.9) | copy-start | bytes 884740
  61.6 4.4 %copy-start.2 = (bf16[1,3,1,128,1152]{4,3,2,1,0:T(8,128)(2,1)S(1)}, bf16[1,3,1,128,1152]{4,3,2,1,0:T(8,128)(2,1)}, u32[]{:S(2)}) copy-start(bf16[1,3,1,128,1152]{4,3,2,1,0:T(8,128)(2,1)} %param.7) | copy-start | bytes 2654212
  61.6 57.5 %all-to-all-start.1 = ((bf16[8,144,640]{2,1,0:T(8,128)(2,1)}), bf16[8,144,640]{2,1,0:T(8,128)(2,1)}, u32[]{:S(2)}, u32[]{:S(2)}) async-start(bf16[8,144,640]{2,1,0:T(8,128)(2,1)} %part_x.1), calls=%async_computation.1 | async-start | bytes 2949120 | tf_op jit(solution)/shard_map/all_to_all | solution.py:216
  71.2 3.9 %collective-permute-start.1 = (bf16[128,1792]{1,0:T(8,128)(2,1)}, bf16[128,1792]{1,0:T(8,128)(2,1)S(1)}, u32[]{:S(2)}, u32[]{:S(2)}) collective-permute-start(bf16[128,1792]{1,0:T(8,128)(2,1)} %get-tuple-element.19.send), channel_id=1, source_target_pairs={{0,1},{1,0},{2,3},{3,2},{4,5},{5,4},{6,7},{7,6},{8,9},{9,8},{10,11... | collective-permute-start | bytes 1376264 | tf_op jit(solution)/shard_map/ppermute | solution.py:238
  75.1 0.8 copy-start.3
  81.8 37.2 %collective-permute-start.8 = (bf16[144,640]{1,0:T(8,128)(2,1)}, bf16[144,640]{1,0:T(8,128)(2,1)S(1)}, u32[]{:S(2)}, u32[]{:S(2)}) collective-permute-start(bf16[144,640]{1,0:T(8,128)(2,1)} %get-tuple-element.26), channel_id=1, source_target_pairs={{0,112},{16,0},{32,16},{48,32},{64,48},{80,64},{96,80},{112,96},{1... | collective-permute-start | bytes 552968 | tf_op jit(solution)/shard_map/ppermute | solution.py:224
  93.8 29.1 %collective-permute-start.7 = (bf16[144,640]{1,0:T(8,128)(2,1)}, bf16[144,640]{1,0:T(8,128)(2,1)S(1)}, u32[]{:S(2)}, u32[]{:S(2)}) collective-permute-start(bf16[144,640]{1,0:T(8,128)(2,1)} %get-tuple-element.27), channel_id=1, source_target_pairs={{0,96},{16,112},{32,0},{48,16},{64,32},{80,48},{96,64},{112,80},{1... | collective-permute-start | bytes 552968 | tf_op jit(solution)/shard_map/ppermute | solution.py:224
  95.8 39.2 %collective-permute-start.6 = (bf16[144,640]{1,0:T(8,128)(2,1)}, bf16[144,640]{1,0:T(8,128)(2,1)S(1)}, u32[]{:S(2)}, u32[]{:S(2)}) collective-permute-start(bf16[144,640]{1,0:T(8,128)(2,1)} %get-tuple-element.28), channel_id=1, source_target_pairs={{0,80},{16,96},{32,112},{48,0},{64,16},{80,32},{96,48},{112,64},{1... | collective-permute-start | bytes 552968 | tf_op jit(solution)/shard_map/ppermute | solution.py:224
  97.7 37.3 %collective-permute-start.5 = (bf16[144,640]{1,0:T(8,128)(2,1)}, bf16[144,640]{1,0:T(8,128)(2,1)S(1)}, u32[]{:S(2)}, u32[]{:S(2)}) collective-permute-start(bf16[144,640]{1,0:T(8,128)(2,1)} %get-tuple-element.29), channel_id=1, source_target_pairs={{0,64},{16,80},{32,96},{48,112},{64,0},{80,16},{96,32},{112,48},{1... | collective-permute-start | bytes 552968 | tf_op jit(solution)/shard_map/ppermute | solution.py:224
  105.5 29.5 %collective-permute-start.4 = (bf16[144,640]{1,0:T(8,128)(2,1)S(1)}, bf16[144,640]{1,0:T(8,128)(2,1)S(1)}, u32[]{:S(2)}, u32[]{:S(2)}) collective-permute-start(bf16[144,640]{1,0:T(8,128)(2,1)S(1)} %get-tuple-element.30), channel_id=1, source_target_pairs={{0,48},{16,64},{32,80},{48,96},{64,112},{80,0},{96,16},{112,32},{1... | collective-permute-start | bytes 552968 | tf_op jit(solution)/shard_map/ppermute | solution.py:224
  119.0 16.0 %collective-permute-start.3 = (bf16[144,640]{1,0:T(8,128)(2,1)S(1)}, bf16[144,640]{1,0:T(8,128)(2,1)S(1)}, u32[]{:S(2)}, u32[]{:S(2)}) collective-permute-start(bf16[144,640]{1,0:T(8,128)(2,1)S(1)} %get-tuple-element.31), channel_id=1, source_target_pairs={{0,32},{16,48},{32,64},{48,80},{64,96},{80,112},{96,0},{112,16},{1... | collective-permute-start | bytes 552968 | tf_op jit(solution)/shard_map/ppermute | solution.py:224
  123.0 17.5 %collective-permute-start.2 = (bf16[144,640]{1,0:T(8,128)(2,1)S(1)}, bf16[144,640]{1,0:T(8,128)(2,1)S(1)}, u32[]{:S(2)}, u32[]{:S(2)}) collective-permute-start(bf16[144,640]{1,0:T(8,128)(2,1)S(1)} %get-tuple-element.25), channel_id=1, source_target_pairs={{0,16},{16,32},{32,48},{48,64},{64,80},{80,96},{96,112},{112,0},{1... | collective-permute-start | bytes 552968 | tf_op jit(solution)/shard_map/ppermute | solution.py:224
  128.7 16.4 %all-to-all-start.2 = ((bf16[8,18,640]{2,1,0:T(8,128)(2,1)}), bf16[8,18,640]{2,1,0:T(8,128)(2,1)S(1)}, u32[]{:S(2)}, u32[]{:S(2)}) async-start(bf16[8,18,640]{2,1,0:T(8,128)(2,1)} %reshape.74), calls=%async_computation.2 | async-start | bytes 491520 | tf_op jit(solution)/shard_map/all_to_all | solution.py:216
  145.1 38.2 %all-to-all-start.3 = ((bf16[16,24,1152]{2,1,0:T(8,128)(2,1)}), bf16[16,24,1152]{2,1,0:T(8,128)(2,1)S(1)}, u32[]{:S(2)}, u32[]{:S(2)}) async-start(bf16[16,24,1152]{2,1,0:T(8,128)(2,1)} %backward.1), calls=%async_computation.3 | async-start | bytes 1769472 | tf_op jit(solution)/shard_map/all_to_all | solution.py:216
  150.1 20.5 %collective-permute-start.15 = (bf16[18,640]{1,0:T(8,128)(2,1)S(1)}, bf16[18,640]{1,0:T(8,128)(2,1)S(1)}, u32[]{:S(2)}, u32[]{:S(2)}) collective-permute-start(bf16[18,640]{1,0:T(8,128)(2,1)S(1)} %get-tuple-element.33), channel_id=1, source_target_pairs={{0,896},{16,912},{32,928},{48,944},{64,960},{80,976},{96,992},{112... | collective-permute-start | bytes 69128 | tf_op jit(solution)/shard_map/ppermute | solution.py:224
  155.3 20.8 %collective-permute-start.14 = (bf16[18,640]{1,0:T(8,128)(2,1)S(1)}, bf16[18,640]{1,0:T(8,128)(2,1)S(1)}, u32[]{:S(2)}, u32[]{:S(2)}) collective-permute-start(bf16[18,640]{1,0:T(8,128)(2,1)S(1)} %get-tuple-element.34), channel_id=1, source_target_pairs={{0,768},{16,784},{32,800},{48,816},{64,832},{80,848},{96,864},{112... | collective-permute-start | bytes 69128 | tf_op jit(solution)/shard_map/ppermute | solution.py:224
  159.6 20.0 %collective-permute-start.13 = (bf16[18,640]{1,0:T(8,128)(2,1)S(1)}, bf16[18,640]{1,0:T(8,128)(2,1)S(1)}, u32[]{:S(2)}, u32[]{:S(2)}) collective-permute-start(bf16[18,640]{1,0:T(8,128)(2,1)S(1)} %get-tuple-element.35), channel_id=1, source_target_pairs={{0,640},{16,656},{32,672},{48,688},{64,704},{80,720},{96,736},{112... | collective-permute-start | bytes 69128 | tf_op jit(solution)/shard_map/ppermute | solution.py:224
  162.9 16.6 %collective-permute-start.12 = (bf16[18,640]{1,0:T(8,128)(2,1)S(1)}, bf16[18,640]{1,0:T(8,128)(2,1)S(1)}, u32[]{:S(2)}, u32[]{:S(2)}) collective-permute-start(bf16[18,640]{1,0:T(8,128)(2,1)S(1)} %get-tuple-element.36), channel_id=1, source_target_pairs={{0,512},{16,528},{32,544},{48,560},{64,576},{80,592},{96,608},{112... | collective-permute-start | bytes 69128 | tf_op jit(solution)/shard_map/ppermute | solution.py:224
  168.4 11.1 %collective-permute-start.11 = (bf16[18,640]{1,0:T(8,128)(2,1)S(1)}, bf16[18,640]{1,0:T(8,128)(2,1)S(1)}, u32[]{:S(2)}, u32[]{:S(2)}) collective-permute-start(bf16[18,640]{1,0:T(8,128)(2,1)S(1)} %get-tuple-element.37), channel_id=1, source_target_pairs={{0,384},{16,400},{32,416},{48,432},{64,448},{80,464},{96,480},{112... | collective-permute-start | bytes 69128 | tf_op jit(solution)/shard_map/ppermute | solution.py:224
  170.6 9.0 %collective-permute-start.10 = (bf16[18,640]{1,0:T(8,128)(2,1)S(1)}, bf16[18,640]{1,0:T(8,128)(2,1)S(1)}, u32[]{:S(2)}, u32[]{:S(2)}) collective-permute-start(bf16[18,640]{1,0:T(8,128)(2,1)S(1)} %get-tuple-element.38), channel_id=1, source_target_pairs={{0,256},{16,272},{32,288},{48,304},{64,320},{80,336},{96,352},{112... | collective-permute-start | bytes 69128 | tf_op jit(solution)/shard_map/ppermute | solution.py:224
  176.1 7.0 %collective-permute-start.9 = (bf16[18,640]{1,0:T(8,128)(2,1)S(1)}, bf16[18,640]{1,0:T(8,128)(2,1)S(1)}, u32[]{:S(2)}, u32[]{:S(2)}) collective-permute-start(bf16[18,640]{1,0:T(8,128)(2,1)S(1)} %get-tuple-element.32), channel_id=1, source_target_pairs={{0,128},{16,144},{32,160},{48,176},{64,192},{80,208},{96,224},{112... | collective-permute-start | bytes 69128 | tf_op jit(solution)/shard_map/ppermute | solution.py:224
  184.1 15.2 %all-to-all-start.4 = ((f32[8,36,72]{2,1,0:T(8,128)}), f32[8,36,72]{2,1,0:T(8,128)S(1)}, u32[]{:S(2)}, u32[]{:S(2)}) async-start(f32[8,36,72]{2,1,0:T(8,128)} %copy.27), calls=%async_computation.4 | async-start | bytes 327680 | tf_op jit(solution)/shard_map/all_to_all | solution.py:216
  (1 other events, 0.8 us)

commit v4 on v1

--- a/solution.py
+++ b/solution.py
@@ -238,8 +238,7 @@
     tokens, width = incoming.shape
     positions = tokens // peers
     side = len(lines(True))
-    x, z = lax.axis_index("dp") // side, lax.axis_index("dp") % side
-    along_x = lambda i, n: (i // side + n) % side * side + i % side
+    z = lax.axis_index("dp") % side
     along_z = lambda i, n: i // side * side + (i % side + n) % side
     blocks = jnp.concatenate([temporal_qkv[0, :, 0], cotangent[0]]).reshape(4, peers, positions, width)
     blocks = jnp.moveaxis(blocks, 1, 0).reshape(peers, 4 * positions, width)
@@ -256,7 +255,8 @@
         name="spatial",
     )(live_counts, near(spatial_qkv[0, :, 0]), near(incoming), spatial_gate)
     part_s = part_of(mine_s, send_s)
-    came_s = shifts(part_s, "dp", x, side, along_x)
+    arrived, _ = lax.optimization_barrier((arrived, part_s))
+    sum_s = lax.psum_scatter(part_s, "dp", scatter_dimension=0, tiled=True, axis_index_groups=lines(True))[0]
     mine_t, send_t = pl.pallas_call(
         forward_kernel,
         in_specs=[SM, VM, VM],
@@ -280,7 +280,7 @@
     came_t, grads = lax.optimization_barrier((came_t, grads))
     home = exchange(grads, "seq")
     sum_t = summed([came_t[i] for i in range(side)])
-    sums = jnp.concatenate([summed(came_s), sum_t], axis=1).astype(jnp.bfloat16)
+    sums = jnp.concatenate([sum_s, sum_t.astype(jnp.bfloat16)], axis=1)
     came = shifts(sums.reshape(side, -1, 2 * HALF), "dp", z, side, along_z)
     both = summed(came).reshape(-1, 2, HALF)
     heads = both[:, :, : HEADS // 2 * HD].reshape(-1, 2, HEADS // 2, HD).transpose(2, 1, 0, 3)

time: 194 us -> 195 us (level)
  the two profiles are of different devices: /device:TPU:14 before, /device:TPU:6 now
where the time goes in v4:
time: 195 us; the launch traced here: 194 us
  waiting for transfers between devices  74.6 us (38%)
  starting transfers between devices  66 us (34%)
  Pallas kernels  28.4 us (15%)
  between operations  14.4 us (7%)
  local copies, waits for them, and re-layouts  6.34 us (3%)
  other arithmetic  3.77 us (2%)
    all_to_all x4, waiting for transfers between devices, exchange(): lax.all_to_all(blocks, axis, split_axis=0, concat_axis=0, tiled=True, axi...  52.1 us
    ppermute x7, starting transfers between devices, shifts(): lax.ppermute(block, axis, [(i, to(i, step)) for i in range(count)])  31.5 us
    all_to_all x4, starting transfers between devices, exchange(): lax.all_to_all(blocks, axis, split_axis=0, concat_axis=0, tiled=True, axi...  28.6 us
    reduce_scatter x1, waiting for transfers between devices, body(): lax.psum_scatter(part_s, 'dp', scatter_dimension=0, tiled=True, axis_inde...  13.7 us
    pallas_call x1, Pallas kernels, body(): pl.pallas_call(backward_kernel, in_specs=[SM, VM, VM, VM], out_specs=VM,...  11.4 us
    pallas_call x2, Pallas kernels, part_of(): pl.pallas_call(part_kernel, in_specs=[VM] * 3, out_specs=VM, out_shape=sh...  6.67 us
    ppermute x2, starting transfers between devices, part_of(): lax.ppermute(send, 'seq', [(i, i ^ 1) for i in range(lax.axis_size('seq'))])  5.89 us
    pallas_call x1, Pallas kernels, body(): pl.pallas_call(spatial_kernel, in_specs=[SM, VM, VM, VM], out_specs=[VM]...  5.2 us
  transfers between devices with their start and end apart: 14, of which 8 were waited for; matrix products, arithmetic and copies ran while one was open for 2% of the time, Pallas kernels for 10%

profile of v4, /device:TPU:6, one launch (start us, length us, event | category | flops | bytes accessed | tf_op | source)
XLA Modules:
  0.0 193.6 jit_solution(11985183033162138835)
XLA Ops:
  8.3 2.1 %maximum_bitcast_fusion = bf16[16,32,1152]{2,1,0:T(8,128)(2,1)} fusion(bf16[1,16,8,1152]{3,2,0,1:T(8,128)(2,1)} %bitcast.44, bf16[1,3,1,128,1152]{4,3,2,1,0:T(8,128)(2,1)S(1)} %copy-done), kind=kLoop, calls=%fused_computation | loop fusion | flops 2359296 | bytes 2359296 | tf_op jit(solution)/shard_map/reshape | solution.py:244
  10.4 7.8 %all-to-all-start = ((bf16[16,32,1152]{2,1,0:T(8,128)(2,1)}), bf16[16,32,1152]{2,1,0:T(8,128)(2,1)S(1)}, u32[]{:S(2)}, u32[]{:S(2)}) async-start(bf16[16,32,1152]{2,1,0:T(8,128)(2,1)} %maximum_bitcast_fusion), calls=%async_computation | async-start | bytes 2359296 | tf_op jit(solution)/shard_map/all_to_all | solution.py:202
  18.2 5.2 %spatial.1 = (bf16[128,640]{1,0:T(8,128)(2,1)}, bf16[128,1792]{1,0:T(8,128)(2,1)}) custom-call(s32[1,2]{1,0:T(1,128)} %counts.5, bf16[3,128,1152]{2,1,0:T(8,128)(2,1)S(1)} %bitcast.46, bf16[128,1152]{1,0:T(8,128)(2,1)S(1)} %bitcast.45, f32[1,1152]{1,0:T(1,128)} %gate.2), custom_call_target="tpu_custom_call" | custom-call | flops 4000000000 | bytes 4000000 | tf_op jit(solution)/shard_map/spatial/pallas_call | solution.py:248
  23.4 2.3 %collective-permute-start = (bf16[128,1792]{1,0:T(8,128)(2,1)}, bf16[128,1792]{1,0:T(8,128)(2,1)S(1)}, u32[]{:S(2)}, u32[]{:S(2)}) collective-permute-start(bf16[128,1792]{1,0:T(8,128)(2,1)} %get-tuple-element.13.send), channel_id=1, source_target_pairs={{0,1},{1,0},{2,3},{3,2},{4,5},{5,4},{6,7},{7,6},{8,9},{9,8},{10,11... | collective-permute-start | bytes 1376264 | tf_op jit(solution)/shard_map/ppermute | solution.py:224
  28.1 3.3 %part.2 = bf16[8,144,640]{2,1,0:T(8,128)(2,1)} custom-call(bf16[128,640]{1,0:T(8,128)(2,1)} %get-tuple-element.12.mine, bf16[128,1792]{1,0:T(8,128)(2,1)} %get-tuple-element.13.send, bf16[128,1792]{1,0:T(8,128)(2,1)} %copy-done.3), custom_call_target="tpu_custom_call" | custom-call | flops 2000000000 | bytes 4000000 | tf_op jit(solution)/shard_map/part/pallas_call | solution.py:225
  31.5 16.1 %all-to-all-done.arrived = bf16[16,32,1152]{2,1,0:T(8,128)(2,1)S(1)} async-done(((bf16[16,32,1152]{2,1,0:T(8,128)(2,1)}), bf16[16,32,1152]{2,1,0:T(8,128)(2,1)S(1)}, u32[]{:S(2)}, u32[]{:S(2)}) %all-to-all-start) | async-done | bytes 1179680 | tf_op jit(solution)/shard_map/all_to_all | solution.py:202
  47.6 5.2 %forward.1 = (bf16[128,640]{1,0:T(8,128)(2,1)}, bf16[128,1792]{1,0:T(8,128)(2,1)}) custom-call(s32[1,2]{1,0:T(1,128)} %counts.5, bf16[16,32,1152]{2,1,0:T(8,128)(2,1)S(1)} %all-to-all-done.arrived, f32[1,1152]{1,0:T(1,128)} %gate.3), custom_call_target="tpu_custom_call" | custom-call | flops 4000000000 | bytes 4000000 | tf_op jit(solution)/shard_map/forward/pallas_call | solution.py:260
  52.7 3.6 %collective-permute-start.1 = (bf16[128,1792]{1,0:T(8,128)(2,1)}, bf16[128,1792]{1,0:T(8,128)(2,1)S(1)}, u32[]{:S(2)}, u32[]{:S(2)}) collective-permute-start(bf16[128,1792]{1,0:T(8,128)(2,1)} %get-tuple-element.16.send), channel_id=1, source_target_pairs={{0,1},{1,0},{2,3},{3,2},{4,5},{5,4},{6,7},{7,6},{8,9},{9,8},{10,11... | collective-permute-start | bytes 1376264 | tf_op jit(solution)/shard_map/ppermute | solution.py:224
  58.7 3.3 %part.3 = bf16[8,144,640]{2,1,0:T(8,128)(2,1)} custom-call(bf16[128,640]{1,0:T(8,128)(2,1)} %get-tuple-element.15.mine, bf16[128,1792]{1,0:T(8,128)(2,1)} %get-tuple-element.16.send, bf16[128,1792]{1,0:T(8,128)(2,1)} %copy-done.4), custom_call_target="tpu_custom_call" | custom-call | flops 2000000000 | bytes 4000000 | tf_op jit(solution)/shard_map/part/pallas_call | solution.py:225
  62.0 13.3 %all-to-all-start.1 = ((bf16[8,144,640]{2,1,0:T(8,128)(2,1)}), bf16[8,144,640]{2,1,0:T(8,128)(2,1)}, u32[]{:S(2)}, u32[]{:S(2)}) async-start(bf16[8,144,640]{2,1,0:T(8,128)(2,1)} %part.3), calls=%async_computation.1 | async-start | bytes 2949120 | tf_op jit(solution)/shard_map/all_to_all | solution.py:202
  76.0 11.4 %backward.1 = bf16[16,24,1152]{2,1,0:T(8,128)(2,1)} custom-call(s32[1,2]{1,0:T(1,128)} %counts.5, bf16[16,32,1152]{2,1,0:T(8,128)(2,1)S(1)} %all-to-all-done.arrived, bf16[128,1792]{1,0:T(8,128)(2,1)} %get-tuple-element.16.send, bf16[1152,1152]{1,0:T(8,128)(2,1)} %proj.1), custom_call_target="tpu_custom_call" | custom-call | flops 8000000000 | bytes 4000000 | tf_op jit(solution)/shard_map/backward/pallas_call | solution.py:271
  87.4 27.6 %all-to-all-done.1 = bf16[8,144,640]{2,1,0:T(8,128)(2,1)} async-done(((bf16[8,144,640]{2,1,0:T(8,128)(2,1)}), bf16[8,144,640]{2,1,0:T(8,128)(2,1)}, u32[]{:S(2)}, u32[]{:S(2)}) %all-to-all-start.1) | async-done | bytes 1474592 | tf_op jit(solution)/shard_map/all_to_all | solution.py:202
  115.0 3.6 %all-to-all-start.2 = ((bf16[16,24,1152]{2,1,0:T(8,128)(2,1)}), bf16[16,24,1152]{2,1,0:T(8,128)(2,1)S(1)}, u32[]{:S(2)}, u32[]{:S(2)}) async-start(bf16[16,24,1152]{2,1,0:T(8,128)(2,1)} %backward.1), calls=%async_computation.2 | async-start | bytes 1769472 | tf_op jit(solution)/shard_map/all_to_all | solution.py:202
  118.8 13.7 %reduce-scatter.2.cloned.1.call-done = bf16[1,144,640]{2,1,0:T(8,128)(2,1)} async-done(((bf16[8,144,640]{2,1,0:T(8,128)(2,1)}), bf16[1,144,640]{2,1,0:T(8,128)(2,1)}) %reduce-scatter.2.cloned.1.call-update) | async-done | bytes 184336 | tf_op jit(solution)/shard_map/reduce_scatter | solution.py:259
  135.3 1.9 collective-permute-start.2
  137.2 10.6 %collective-permute-start.8 = (bf16[18,1280]{1,0:T(8,128)(2,1)S(1)}, bf16[18,1280]{1,0:T(8,128)(2,1)S(1)}, u32[]{:S(2)}, u32[]{:S(2)}) collective-permute-start(bf16[18,1280]{1,0:T(8,128)(2,1)S(1)} %get-tuple-element.22), channel_id=1, source_target_pairs={{0,112},{16,0},{32,16},{48,32},{64,48},{80,64},{96,80},{112,96},{1... | collective-permute-start | bytes 138248 | tf_op jit(solution)/shard_map/ppermute | solution.py:210
  147.8 3.4 %collective-permute-start.7 = (bf16[18,1280]{1,0:T(8,128)(2,1)S(1)}, bf16[18,1280]{1,0:T(8,128)(2,1)S(1)}, u32[]{:S(2)}, u32[]{:S(2)}) collective-permute-start(bf16[18,1280]{1,0:T(8,128)(2,1)S(1)} %get-tuple-element.23), channel_id=1, source_target_pairs={{0,96},{16,112},{32,0},{48,16},{64,32},{80,48},{96,64},{112,80},{1... | collective-permute-start | bytes 138248 | tf_op jit(solution)/shard_map/ppermute | solution.py:210
  151.2 1.9 collective-permute-start.6
  153.1 8.4 %collective-permute-start.5 = (bf16[18,1280]{1,0:T(8,128)(2,1)S(1)}, bf16[18,1280]{1,0:T(8,128)(2,1)S(1)}, u32[]{:S(2)}, u32[]{:S(2)}) collective-permute-start(bf16[18,1280]{1,0:T(8,128)(2,1)S(1)} %get-tuple-element.25), channel_id=1, source_target_pairs={{0,64},{16,80},{32,96},{48,112},{64,0},{80,16},{96,32},{112,48},{1... | collective-permute-start | bytes 138248 | tf_op jit(solution)/shard_map/ppermute | solution.py:210
  161.5 1.9 collective-permute-start.4
  163.5 3.4 %collective-permute-start.3 = (bf16[18,1280]{1,0:T(8,128)(2,1)S(1)}, bf16[18,1280]{1,0:T(8,128)(2,1)S(1)}, u32[]{:S(2)}, u32[]{:S(2)}) collective-permute-start(bf16[18,1280]{1,0:T(8,128)(2,1)S(1)} %get-tuple-element.27), channel_id=1, source_target_pairs={{0,32},{16,48},{32,64},{48,80},{64,96},{80,112},{96,0},{112,16},{1... | collective-permute-start | bytes 138248 | tf_op jit(solution)/shard_map/ppermute | solution.py:210
  166.9 3.9 %collective-permute-done.4 = bf16[18,1280]{1,0:T(8,128)(2,1)S(1)} collective-permute-done((bf16[18,1280]{1,0:T(8,128)(2,1)S(1)}, bf16[18,1280]{1,0:T(8,128)(2,1)S(1)}, u32[]{:S(2)}, u32[]{:S(2)}) %collective-permute-start.4) | collective-permute-done | bytes 46112 | tf_op jit(solution)/shard_map/ppermute | solution.py:210
  172.7 4.0 %all-to-all-start.3 = ((f32[8,36,72]{2,1,0:T(8,128)}), f32[8,36,72]{2,1,0:T(8,128)S(1)}, u32[]{:S(2)}, u32[]{:S(2)}) async-start(f32[8,36,72]{2,1,0:T(8,128)} %copy.25), calls=%async_computation.4 | async-start | bytes 327680 | tf_op jit(solution)/shard_map/all_to_all | solution.py:202
  177.6 8.4 %all-to-all-done.3 = f32[8,36,72]{2,1,0:T(8,128)S(1)} async-done(((f32[8,36,72]{2,1,0:T(8,128)}), f32[8,36,72]{2,1,0:T(8,128)S(1)}, u32[]{:S(2)}, u32[]{:S(2)}) %all-to-all-start.3) | async-done | bytes 82976 | tf_op jit(solution)/shard_map/all_to_all | solution.py:202
  (35 shorter events, 13.0 us)
Async XLA Ops:
  7.2 1.2 copy-start
  10.4 7.8 %copy-start.1 = (bf16[1,1,128,1152]{3,2,1,0:T(8,128)(2,1)S(1)}, bf16[1,1,128,1152]{3,2,1,0:T(8,128)(2,1)}, u32[]{:S(2)}) copy-start(bf16[1,1,128,1152]{3,2,1,0:T(8,128)(2,1)} %param.9) | copy-start | bytes 884740
  10.4 7.8 %copy-start.2 = (bf16[1,3,1,128,1152]{4,3,2,1,0:T(8,128)(2,1)S(1)}, bf16[1,3,1,128,1152]{4,3,2,1,0:T(8,128)(2,1)}, u32[]{:S(2)}) copy-start(bf16[1,3,1,128,1152]{4,3,2,1,0:T(8,128)(2,1)} %param.7) | copy-start | bytes 2654212
  10.4 37.1 %all-to-all-start = ((bf16[16,32,1152]{2,1,0:T(8,128)(2,1)}), bf16[16,32,1152]{2,1,0:T(8,128)(2,1)S(1)}, u32[]{:S(2)}, u32[]{:S(2)}) async-start(bf16[16,32,1152]{2,1,0:T(8,128)(2,1)} %maximum_bitcast_fusion), calls=%async_computation | async-start | bytes 2359296 | tf_op jit(solution)/shard_map/all_to_all | solution.py:202
  23.4 3.9 %collective-permute-start = (bf16[128,1792]{1,0:T(8,128)(2,1)}, bf16[128,1792]{1,0:T(8,128)(2,1)S(1)}, u32[]{:S(2)}, u32[]{:S(2)}) collective-permute-start(bf16[128,1792]{1,0:T(8,128)(2,1)} %get-tuple-element.13.send), channel_id=1, source_target_pairs={{0,1},{1,0},{2,3},{3,2},{4,5},{5,4},{6,7},{7,6},{8,9},{9,8},{10,11... | collective-permute-start | bytes 1376264 | tf_op jit(solution)/shard_map/ppermute | solution.py:224
  27.4 0.8 copy-start.3
  52.7 5.2 %collective-permute-start.1 = (bf16[128,1792]{1,0:T(8,128)(2,1)}, bf16[128,1792]{1,0:T(8,128)(2,1)S(1)}, u32[]{:S(2)}, u32[]{:S(2)}) collective-permute-start(bf16[128,1792]{1,0:T(8,128)(2,1)} %get-tuple-element.16.send), channel_id=1, source_target_pairs={{0,1},{1,0},{2,3},{3,2},{4,5},{5,4},{6,7},{7,6},{8,9},{9,8},{10,11... | collective-permute-start | bytes 1376264 | tf_op jit(solution)/shard_map/ppermute | solution.py:224
  57.9 0.8 copy-start.4
  62.0 52.9 %all-to-all-start.1 = ((bf16[8,144,640]{2,1,0:T(8,128)(2,1)}), bf16[8,144,640]{2,1,0:T(8,128)(2,1)}, u32[]{:S(2)}, u32[]{:S(2)}) async-start(bf16[8,144,640]{2,1,0:T(8,128)(2,1)} %part.3), calls=%async_computation.1 | async-start | bytes 2949120 | tf_op jit(solution)/shard_map/all_to_all | solution.py:202
  75.3 57.2 %reduce-scatter.2.cloned.1.call-start = ((), (), s32[]{:S(2)}) async-start(), calls=%async_computation.5 | async-start | bytes 1658880 | tf_op jit(solution)/shard_map/reduce_scatter | solution.py:259
  115.0 57.0 %all-to-all-start.2 = ((bf16[16,24,1152]{2,1,0:T(8,128)(2,1)}), bf16[16,24,1152]{2,1,0:T(8,128)(2,1)S(1)}, u32[]{:S(2)}, u32[]{:S(2)}) async-start(bf16[16,24,1152]{2,1,0:T(8,128)(2,1)} %backward.1), calls=%async_computation.2 | async-start | bytes 1769472 | tf_op jit(solution)/shard_map/all_to_all | solution.py:202
  135.3 26.2 %collective-permute-start.2 = (bf16[18,1280]{1,0:T(8,128)(2,1)S(1)}, bf16[18,1280]{1,0:T(8,128)(2,1)S(1)}, u32[]{:S(2)}, u32[]{:S(2)}) collective-permute-start(bf16[18,1280]{1,0:T(8,128)(2,1)S(1)} %get-tuple-element.21), channel_id=1, source_target_pairs={{0,16},{16,32},{32,48},{48,64},{64,80},{80,96},{96,112},{112,0},{1... | collective-permute-start | bytes 138248 | tf_op jit(solution)/shard_map/ppermute | solution.py:210
  137.2 26.2 %collective-permute-start.8 = (bf16[18,1280]{1,0:T(8,128)(2,1)S(1)}, bf16[18,1280]{1,0:T(8,128)(2,1)S(1)}, u32[]{:S(2)}, u32[]{:S(2)}) collective-permute-start(bf16[18,1280]{1,0:T(8,128)(2,1)S(1)} %get-tuple-element.22), channel_id=1, source_target_pairs={{0,112},{16,0},{32,16},{48,32},{64,48},{80,64},{96,80},{112,96},{1... | collective-permute-start | bytes 138248 | tf_op jit(solution)/shard_map/ppermute | solution.py:210
  147.8 19.0 %collective-permute-start.7 = (bf16[18,1280]{1,0:T(8,128)(2,1)S(1)}, bf16[18,1280]{1,0:T(8,128)(2,1)S(1)}, u32[]{:S(2)}, u32[]{:S(2)}) collective-permute-start(bf16[18,1280]{1,0:T(8,128)(2,1)S(1)} %get-tuple-element.23), channel_id=1, source_target_pairs={{0,96},{16,112},{32,0},{48,16},{64,32},{80,48},{96,64},{112,80},{1... | collective-permute-start | bytes 138248 | tf_op jit(solution)/shard_map/ppermute | solution.py:210
  151.2 15.7 %collective-permute-start.6 = (bf16[18,1280]{1,0:T(8,128)(2,1)S(1)}, bf16[18,1280]{1,0:T(8,128)(2,1)S(1)}, u32[]{:S(2)}, u32[]{:S(2)}) collective-permute-start(bf16[18,1280]{1,0:T(8,128)(2,1)S(1)} %get-tuple-element.24), channel_id=1, source_target_pairs={{0,80},{16,96},{32,112},{48,0},{64,16},{80,32},{96,48},{112,64},{1... | collective-permute-start | bytes 138248 | tf_op jit(solution)/shard_map/ppermute | solution.py:210
  153.1 13.7 %collective-permute-start.5 = (bf16[18,1280]{1,0:T(8,128)(2,1)S(1)}, bf16[18,1280]{1,0:T(8,128)(2,1)S(1)}, u32[]{:S(2)}, u32[]{:S(2)}) collective-permute-start(bf16[18,1280]{1,0:T(8,128)(2,1)S(1)} %get-tuple-element.25), channel_id=1, source_target_pairs={{0,64},{16,80},{32,96},{48,112},{64,0},{80,16},{96,32},{112,48},{1... | collective-permute-start | bytes 138248 | tf_op jit(solution)/shard_map/ppermute | solution.py:210
  161.5 9.2 %collective-permute-start.4 = (bf16[18,1280]{1,0:T(8,128)(2,1)S(1)}, bf16[18,1280]{1,0:T(8,128)(2,1)S(1)}, u32[]{:S(2)}, u32[]{:S(2)}) collective-permute-start(bf16[18,1280]{1,0:T(8,128)(2,1)S(1)} %get-tuple-element.26), channel_id=1, source_target_pairs={{0,48},{16,64},{32,80},{48,96},{64,112},{80,0},{96,16},{112,32},{1... | collective-permute-start | bytes 138248 | tf_op jit(solution)/shard_map/ppermute | solution.py:210
  163.5 8.2 %collective-permute-start.3 = (bf16[18,1280]{1,0:T(8,128)(2,1)S(1)}, bf16[18,1280]{1,0:T(8,128)(2,1)S(1)}, u32[]{:S(2)}, u32[]{:S(2)}) collective-permute-start(bf16[18,1280]{1,0:T(8,128)(2,1)S(1)} %get-tuple-element.27), channel_id=1, source_target_pairs={{0,32},{16,48},{32,64},{48,80},{64,96},{80,112},{96,0},{112,16},{1... | collective-permute-start | bytes 138248 | tf_op jit(solution)/shard_map/ppermute | solution.py:210
  172.7 13.4 %all-to-all-start.3 = ((f32[8,36,72]{2,1,0:T(8,128)}), f32[8,36,72]{2,1,0:T(8,128)S(1)}, u32[]{:S(2)}, u32[]{:S(2)}) async-start(f32[8,36,72]{2,1,0:T(8,128)} %copy.25), calls=%async_computation.4 | async-start | bytes 327680 | tf_op jit(solution)/shard_map/all_to_all | solution.py:202
Sparse Core Ops, SparseCore 0:
  79.5 52.9 reduce-scatter.1
